TPU v7x, 32 devices: a whole 2x2x4 slice. The times are simulated.
32 devices in a mesh: lat: 8 (over y, x, core), lon: 4 (over z).
Axes of the slice: x: 2, y: 2, z: 4, core: 2. Of those that a mesh axis runs over, the one named last changes fastest.
Arguments:
- fields: float32 [4, 6, 256, 1280], P(None, None, 'lat', 'lon'), may hold values from -6 to 6
- dep_row: int32 [6, 256, 1280], P(None, 'lat', 'lon'), may hold values from -4 to 255, as said below
- dep_col: int32 [6, 256, 1280], P(None, 'lat', 'lon'), may hold values from 0 to 1279, as said below
- weights: float32 [8, 6, 256, 1280], P(None, None, 'lat', 'lon'), may hold values from -0.25 to 0.75
Outputs:
- departed: float32 [4, 6, 256, 1280], P(None, None, 'lat', 'lon')
Inputs may be any that keep to these rules, and one draw needn't show every extreme that they name: dep_row[l, i, j] lies within i - 4 to i. dep_col[l, i, j] equals (j + k) modulo 1280 for some k from -4 to 0.
All inputs are finite; a program needn't handle non-finite values.
Results may differ from a plain program's by a relative error of at most 0.0003.
Values sent between devices are 32-bit elements; how exact they have to be, the bound alone decides.
No kernel may reach another device: no remote copies, remote signals or barrier semaphores. Data moves between devices by JAX's collectives and lax.ppermute only.
A program may use at most 64 MiB of HBM per device.

v0:
```python
import jax
import jax.numpy as jnp
from jax import lax
from jax.sharding import PartitionSpec as P

HALO = 4


def padded_2(x, sides, width, wrap):
    for axis, dim in sides:
        devices, length = (lax.axis_size(axis), x.shape[dim])
        up = [(i, (i + 1) % devices) for i in range(devices if wrap else devices - 1)]
        down = [(j, i) for i, j in up]
        last = lax.slice_in_dim(x, length - width, length, axis=dim)
        leading = lax.slice_in_dim(x, 0, width, axis=dim)
        before = lax.ppermute(last, axis, up)
        after = lax.ppermute(leading, axis, down)
        x = jnp.concatenate([before, x, after], axis=dim)
    return x


def swapped(x, axis, stride):
    return lax.ppermute(x, axis, [(i, i ^ 1 << stride) for i in range(lax.axis_size(axis))])


def body(fields, dep_row, dep_col, weights):
    nfield, nlev, rows_here, cols_here = fields.shape
    lat_count = lax.axis_size("lat")
    lon_count = lax.axis_size("lon")
    band = lax.axis_index("lat")
    sector = lax.axis_index("lon")
    wide = padded_2(fields, (("lon", 3),), HALO, True)
    padded = padded_2(wide, (("lat", 2),), HALO, False)
    outgoing = jnp.where(band == 0, wide[:, :, :HALO], wide[:, :, rows_here - HALO :])
    partner = swapped(outgoing, "lon", lon_count.bit_length() - 2)
    flipped = partner[:, :, ::-1]
    north = jnp.where(band == 0, flipped, padded[:, :, :HALO])
    south = jnp.where(band == lat_count - 1, flipped, padded[:, :, rows_here + HALO :])
    padded = jnp.concatenate([north, padded[:, :, HALO : rows_here + HALO], south], axis=2)
    total_cols = cols_here * lon_count
    shape = (nlev, rows_here, cols_here)
    row_global = band * rows_here + lax.broadcasted_iota(jnp.int32, shape, 1)
    col_global = sector * cols_here + lax.broadcasted_iota(jnp.int32, shape, 2)
    offset_row = dep_row - row_global
    offset_col = jnp.mod(dep_col - col_global + HALO, total_cols) - HALO
    col_select = []
    row_select = []
    for shift in range(2 * HALO):
        col_term = jnp.zeros(shape, jnp.float32)
        row_term = jnp.zeros(shape, jnp.float32)
        for step in range(4):
            col_term = col_term + jnp.where(
                offset_col + step == shift - HALO, weights[4 + step], 0.0
            )
            row_term = row_term + jnp.where(offset_row + step == shift - HALO, weights[step], 0.0)
        col_select.append(col_term)
        row_select.append(row_term)
    total = jnp.zeros(fields.shape, jnp.float32)
    for row_shift in range(2 * HALO):
        band_rows = padded[:, :, row_shift : row_shift + rows_here]
        line = jnp.zeros(fields.shape, jnp.float32)
        for col_shift in range(2 * HALO):
            line = (
                line + col_select[col_shift] * band_rows[:, :, :, col_shift : col_shift + cols_here]
            )
        total = total + row_select[row_shift] * line
    return total


def solution(mesh):
    return jax.shard_map(
        body,
        mesh=mesh,
        in_specs=(
            P(None, None, "lat", "lon"),
            P(None, "lat", "lon"),
            P(None, "lat", "lon"),
            P(None, None, "lat", "lon"),
        ),
        out_specs=P(None, None, "lat", "lon"),
        check_vma=False,
    )
```

profile of v0, /device:TPU:3, one launch (start us, length us, event | category | flops | bytes accessed | tf_op | source)
XLA Modules:
  0.0 63.1 jit_solution(10448569810515244594)
XLA Ops:
  0.0 2.2 %fusion.131 = (f32[4,6,32,4]{3,2,1,0:T(8,128)}, f32[4,6,32,4]{3,2,1,0:T(8,128)}) fusion(f32[4,6,32,320]{3,2,1,0:T(8,128)} %param.4), kind=kLoop, calls=%fused_computation.271 | loop fusion | bytes 49152 | tf_op jit(solution)/shard_map/slice | solution.py:14
  2.2 1.3 %collective-permute-start = (f32[4,6,32,4]{3,2,1,0:T(8,128)}, f32[4,6,32,4]{3,2,1,0:T(8,128)}, u32[]{:S(2)}, u32[]{:S(2)}) collective-permute-start(f32[4,6,32,4]{3,2,1,0:T(8,128)} %get-tuple-element.26), channel_id=1, source_target_pairs={{0,1},{1,2},{2,3},{3,0},{4,5},{5,6},{6,7},{7,4},{8,9},{9,10},{10,1... | collective-permute-start | bytes 36872 | tf_op jit(solution)/shard_map/ppermute | solution.py:16
  3.5 2.0 %collective-permute-start.1 = (f32[4,6,32,4]{3,2,1,0:T(8,128)}, f32[4,6,32,4]{3,2,1,0:T(8,128)}, u32[]{:S(2)}, u32[]{:S(2)}) collective-permute-start(f32[4,6,32,4]{3,2,1,0:T(8,128)} %get-tuple-element.27), channel_id=1, source_target_pairs={{1,0},{2,1},{3,2},{0,3},{5,4},{6,5},{7,6},{4,7},{9,8},{10,9},{11,1... | collective-permute-start | bytes 36872 | tf_op jit(solution)/shard_map/ppermute | solution.py:17
  5.5 0.0 copy-done.4
  5.5 3.1 %fusion.83 = (f32[6,32,320]{2,1,0:T(8,128)}, f32[6,32,320]{2,1,0:T(8,128)}, f32[6,32,320]{2,1,0:T(8,128)}, f32[6,32,320]{2,1,0:T(8,128)}) fusion(f32[8,6,32,320]{3,2,1,0:T(8,128)} %param.7, s32[6,32,320]{2,1,0:T(8,128)S(1)} %copy-done.4, s32[320]{0:T(512)S(1)} %iota_add_fusion), kind=kLoop, calls=%fused_computation.158 | loop fusion | flops 3440640 | bytes 2213120 | tf_op jit(solution)/shard_map/add | solution.py:52
  8.6 0.0 copy-done.1
  8.6 1.7 %fusion.84 = (f32[6,32,320]{2,1,0:T(8,128)}, f32[6,32,320]{2,1,0:T(8,128)}, f32[6,32,320]{2,1,0:T(8,128)}, f32[6,32,320]{2,1,0:T(8,128)}) fusion(f32[8,6,32,320]{3,2,1,0:T(8,128)S(1)} %copy-done.1, s32[6,32,320]{2,1,0:T(8,128)S(1)} %copy-done.4, s32[320]{0:T(512)S(1)} %iota_add_fusion), kind=kLoop, calls=%fused_computation.159 | loop fusion | flops 3440640 | bytes 2213120 | tf_op jit(solution)/shard_map/add | solution.py:52
  10.2 2.6 %fusion.108 = (f32[6,32,320]{2,1,0:T(8,128)}, f32[6,32,320]{2,1,0:T(8,128)}, f32[6,32,320]{2,1,0:T(8,128)}, f32[6,32,320]{2,1,0:T(8,128)}) fusion(f32[8,6,32,320]{3,2,1,0:T(8,128)S(1)} %copy-done.1, s32[6,32,320]{2,1,0:T(8,128)} %param.5, s32[32]{0:T(128)S(1)} %iota_add_fusion.1), kind=kLoop, calls=%fused_computation.215 | loop fusion | flops 2949120 | bytes 2211968 | tf_op jit(solution)/shard_map/add | solution.py:55
  12.8 1.6 %collective-permute-done = f32[4,6,32,4]{3,2,1,0:T(8,128)} collective-permute-done((f32[4,6,32,4]{3,2,1,0:T(8,128)}, f32[4,6,32,4]{3,2,1,0:T(8,128)}, u32[]{:S(2)}, u32[]{:S(2)}) %collective-permute-start) | collective-permute-done | bytes 12320 | tf_op jit(solution)/shard_map/ppermute | solution.py:16
  14.4 8.2 %collective-permute-done.1 = f32[4,6,32,4]{3,2,1,0:T(8,128)} collective-permute-done((f32[4,6,32,4]{3,2,1,0:T(8,128)}, f32[4,6,32,4]{3,2,1,0:T(8,128)}, u32[]{:S(2)}, u32[]{:S(2)}) %collective-permute-start.1) | collective-permute-done | bytes 12320 | tf_op jit(solution)/shard_map/ppermute | solution.py:17
  22.7 0.0 copy-done
  22.7 2.1 %broadcast_select_fusion.2 = (f32[4,6,4,328]{3,2,1,0:T(4,128)}, f32[4,6,4,328]{3,2,1,0:T(4,128)}, f32[4,6,4,328]{3,2,1,0:T(4,128)}) fusion(pred[]{:T(512)S(6)} %eq.209, f32[4,6,32,4]{3,2,1,0:T(8,128)} %collective-permute-done.1, f32[4,6,32,320]{3,2,1,0:T(8,128)S(1)} %copy-done, f32[4,6,32,4]{3,2,1,0:T(8,128)} %collective-permute-done), kind=kLoop, calls=%fused_computation.268 | loop fusion | flops 157440 | bytes 1385473 | tf_op jit(solution)/shard_map/jit(_where)/select_n | solution.py:34
  24.7 0.5 collective-permute-start.2
  25.2 4.9 %collective-permute-start.3 = (f32[4,6,4,328]{3,2,1,0:T(4,128)}, f32[4,6,4,328]{3,2,1,0:T(4,128)S(1)}, u32[]{:S(2)}, u32[]{:S(2)}) collective-permute-start(f32[4,6,4,328]{3,2,1,0:T(4,128)} %get-tuple-element.6), channel_id=1, source_target_pairs={{0,4},{4,8},{8,12},{12,16},{16,20},{20,24},{24,28},{1,5},{5,9},{9,... | collective-permute-start | bytes 377864 | tf_op jit(solution)/shard_map/ppermute | solution.py:16
  30.1 1.9 %collective-permute-start.4 = (f32[4,6,4,328]{3,2,1,0:T(4,128)}, f32[4,6,4,328]{3,2,1,0:T(4,128)S(1)}, u32[]{:S(2)}, u32[]{:S(2)}) collective-permute-start(f32[4,6,4,328]{3,2,1,0:T(4,128)} %get-tuple-element.7), channel_id=1, source_target_pairs={{4,0},{8,4},{12,8},{16,12},{20,16},{24,20},{28,24},{5,1},{9,5},{13... | collective-permute-start | bytes 377864 | tf_op jit(solution)/shard_map/ppermute | solution.py:17
  32.0 0.0 copy-done.5
  32.0 1.6 %fusion.107 = (f32[6,32,320]{2,1,0:T(8,128)}, f32[6,32,320]{2,1,0:T(8,128)}, f32[6,32,320]{2,1,0:T(8,128)}, f32[6,32,320]{2,1,0:T(8,128)}) fusion(f32[8,6,32,320]{3,2,1,0:T(8,128)S(1)} %copy-done.1, s32[6,32,320]{2,1,0:T(8,128)S(1)} %copy-done.5, s32[32]{0:T(128)S(1)} %iota_add_fusion.1), kind=kLoop, calls=%fused_computation.214 | loop fusion | flops 2949120 | bytes 2211968 | tf_op jit(solution)/shard_map/add | solution.py:55
  33.6 0.1 collective-permute-done.2
  33.7 0.3 rev.3
  33.9 0.0 collective-permute-done.3
  33.9 3.7 %collective-permute-done.4 = f32[4,6,4,328]{3,2,1,0:T(4,128)S(1)} collective-permute-done((f32[4,6,4,328]{3,2,1,0:T(4,128)}, f32[4,6,4,328]{3,2,1,0:T(4,128)S(1)}, u32[]{:S(2)}, u32[]{:S(2)}) %collective-permute-start.4) | collective-permute-done | bytes 125984 | tf_op jit(solution)/shard_map/ppermute | solution.py:17
  37.7 0.0 copy-start.2
  37.7 3.1 %maximum_maximum_fusion = (f32[4,6,36,328]{3,2,1,0:T(8,128)S(1)}, f32[4,6,36,328]{3,2,1,0:T(8,128)S(1)}) fusion(f32[4,6,32,4]{3,2,1,0:T(8,128)} %collective-permute-done.1, f32[4,6,32,320]{3,2,1,0:T(8,128)} %param.4, f32[4,6,32,4]{3,2,1,0:T(8,128)} %collective-permute-done, f32[4,6,4,328]{3,2,1,0:T(4,128)S(1)} %bitcast.269, f32[4,6,4,328]{3,2,1,0:T(4,128)S(1)} %bitcast.270), kind=kLoop, calls=%fused_computation.5 | loop fusion | flops 1700352 | bytes 3526656 | tf_op jit(solution)/shard_map/concatenate | solution.py:39
  40.9 22.3 %fusion.8 = f32[4,6,32,320]{3,2,1,0:T(8,128)} fusion(f32[4,6,32,4]{3,2,1,0:T(8,128)} %collective-permute-done.1, f32[4,6,32,4]{3,2,1,0:T(8,128)} %collective-permute-done, f32[4,6,36,328]{3,2,1,0:T(8,128)S(1)} %get-tuple-element.25, f32[4,6,32,320]{3,2,1,0:T(8,128)} %param.4, f32[4,6,36,328]{3,2,1,0:T(8,128)S(1)} %get-tuple-element.24, ...), kind=kLoop, calls=%fused_computation.15 | loop fusion | flops 34897920 | bytes 60973056 | tf_op jit(solution)/shard_map/add | solution.py:66
  (10 shorter events, 0.0 us)
Async XLA Ops:
  0.0 5.5 %copy-start.4 = (s32[6,32,320]{2,1,0:T(8,128)S(1)}, s32[6,32,320]{2,1,0:T(8,128)}, u32[]{:S(2)}) copy-start(s32[6,32,320]{2,1,0:T(8,128)} %param.6) | copy-start | bytes 737284
  2.2 12.3 %collective-permute-start = (f32[4,6,32,4]{3,2,1,0:T(8,128)}, f32[4,6,32,4]{3,2,1,0:T(8,128)}, u32[]{:S(2)}, u32[]{:S(2)}) collective-permute-start(f32[4,6,32,4]{3,2,1,0:T(8,128)} %get-tuple-element.26), channel_id=1, source_target_pairs={{0,1},{1,2},{2,3},{3,0},{4,5},{5,6},{6,7},{7,4},{8,9},{9,10},{10,1... | collective-permute-start | bytes 36872 | tf_op jit(solution)/shard_map/ppermute | solution.py:16
  3.5 19.2 %collective-permute-start.1 = (f32[4,6,32,4]{3,2,1,0:T(8,128)}, f32[4,6,32,4]{3,2,1,0:T(8,128)}, u32[]{:S(2)}, u32[]{:S(2)}) collective-permute-start(f32[4,6,32,4]{3,2,1,0:T(8,128)} %get-tuple-element.27), channel_id=1, source_target_pairs={{1,0},{2,1},{3,2},{0,3},{5,4},{6,5},{7,6},{4,7},{9,8},{10,9},{11,1... | collective-permute-start | bytes 36872 | tf_op jit(solution)/shard_map/ppermute | solution.py:17
  5.5 3.1 %copy-start.1 = (f32[8,6,32,320]{3,2,1,0:T(8,128)S(1)}, f32[8,6,32,320]{3,2,1,0:T(8,128)}, u32[]{:S(2)}) copy-start(f32[8,6,32,320]{3,2,1,0:T(8,128)} %param.7) | copy-start | bytes 5898244
  10.2 12.4 %copy-start = (f32[4,6,32,320]{3,2,1,0:T(8,128)S(1)}, f32[4,6,32,320]{3,2,1,0:T(8,128)}, u32[]{:S(2)}) copy-start(f32[4,6,32,320]{3,2,1,0:T(8,128)} %param.4) | copy-start | bytes 2949124
  12.8 19.2 %copy-start.5 = (s32[6,32,320]{2,1,0:T(8,128)S(1)}, s32[6,32,320]{2,1,0:T(8,128)}, u32[]{:S(2)}) copy-start(s32[6,32,320]{2,1,0:T(8,128)} %param.5) | copy-start | bytes 737284
  24.7 8.9 %collective-permute-start.2 = (f32[4,6,4,328]{3,2,1,0:T(4,128)}, f32[4,6,4,328]{3,2,1,0:T(4,128)S(1)}, u32[]{:S(2)}, u32[]{:S(2)}) collective-permute-start(f32[4,6,4,328]{3,2,1,0:T(4,128)} %get-tuple-element.5), channel_id=1, source_target_pairs={{0,2},{1,3},{2,0},{3,1},{4,6},{5,7},{6,4},{7,5},{8,10},{9,11},{10,... | collective-permute-start | bytes 377864 | tf_op jit(solution)/shard_map/ppermute | solution.py:23
  25.2 8.7 %collective-permute-start.3 = (f32[4,6,4,328]{3,2,1,0:T(4,128)}, f32[4,6,4,328]{3,2,1,0:T(4,128)S(1)}, u32[]{:S(2)}, u32[]{:S(2)}) collective-permute-start(f32[4,6,4,328]{3,2,1,0:T(4,128)} %get-tuple-element.6), channel_id=1, source_target_pairs={{0,4},{4,8},{8,12},{12,16},{16,20},{20,24},{24,28},{1,5},{5,9},{9,... | collective-permute-start | bytes 377864 | tf_op jit(solution)/shard_map/ppermute | solution.py:16
  30.1 7.6 %collective-permute-start.4 = (f32[4,6,4,328]{3,2,1,0:T(4,128)}, f32[4,6,4,328]{3,2,1,0:T(4,128)S(1)}, u32[]{:S(2)}, u32[]{:S(2)}) collective-permute-start(f32[4,6,4,328]{3,2,1,0:T(4,128)} %get-tuple-element.7), channel_id=1, source_target_pairs={{4,0},{8,4},{12,8},{16,12},{20,16},{24,20},{28,24},{5,1},{9,5},{13... | collective-permute-start | bytes 377864 | tf_op jit(solution)/shard_map/ppermute | solution.py:17
  37.7 3.1 %copy-start.2 = (f32[6,32,320]{2,1,0:T(8,128)S(1)}, f32[6,32,320]{2,1,0:T(8,128)}, u32[]{:S(2)}) copy-start(f32[6,32,320]{2,1,0:T(8,128)} %get-tuple-element.8) | copy-start | bytes 737284
  37.7 3.1 %copy-start.3 = (f32[6,32,320]{2,1,0:T(8,128)S(1)}, f32[6,32,320]{2,1,0:T(8,128)}, u32[]{:S(2)}) copy-start(f32[6,32,320]{2,1,0:T(8,128)} %get-tuple-element.9) | copy-start | bytes 737284
where the time goes:
time: 63.4 us; the launch traced here: 63.1 us
  other arithmetic  36.4 us (57%)
  waiting for transfers between devices  13.6 us (21%)
  starting transfers between devices  10.6 us (17%)
  local copies, waits for them, and re-layouts  2.45 us (4%)
    add x1, other arithmetic, body(): total = total + row_select[row_shift] * line  22.3 us
    ppermute x2, waiting for transfers between devices, padded_2(): after = lax.ppermute(leading, axis, down)  12 us
    ppermute x2, starting transfers between devices, padded_2(): before = lax.ppermute(last, axis, up)  6.17 us
    add x2, other arithmetic, body(): col_term + jnp.where(offset_col + step == shift - HALO, weights[4 + step]...  4.73 us
    add x2, other arithmetic, body(): row_term + jnp.where(offset_row + step == shift - HALO, weights[step], 0.0)  4.18 us
    ppermute x2, starting transfers between devices, padded_2(): after = lax.ppermute(leading, axis, down)  3.95 us
    concatenate x1, other arithmetic, body(): jnp.concatenate([north, padded[:, :, HALO:rows_here + HALO], south], axis=2)  3.11 us
    slice x1, local copies, waits for them, and re-layouts, padded_2(): last = lax.slice_in_dim(x, length - width, length, axis=dim)  2.16 us
  transfers between devices with their start and end apart: 5, of which 4 were waited for; matrix products, arithmetic and copies ran while one was open for 15% of the time, Pallas kernels for 0%

commit v1 on v0

v1 whole, which is shorter than its diff:
```python
import jax
import jax.numpy as jnp
from jax import lax
from jax.experimental import pallas as pl
from jax.experimental.pallas import tpu as pltpu
from jax.sharding import PartitionSpec as P

HALO = 4
TAPS = 2 * HALO
LANES = 128
SUB = 8
VMEM = 48 * 1024 * 1024


def iota(dim):
    return lax.broadcasted_iota(jnp.int32, (SUB, LANES), dim)


def expand(k, w):
    masks = [k == v for v in range(HALO + 1)]
    out = []
    for t in range(TAPS):
        val = jnp.zeros((SUB, LANES), jnp.float32)
        for v in range(HALO + 1):
            if 0 <= t - v < 4:
                val = jnp.where(masks[v], w[t - v], val)
        out.append(val)
    return out


def shifted(prev, cur, nxt, t):
    lane = iota(1)
    if t < HALO:
        d = HALO - t
        return pltpu.roll(jnp.where(lane >= LANES - d, prev, cur), d, 1)
    if t == HALO:
        return cur
    e = t - HALO
    z = cur if nxt is None else jnp.where(lane < e, nxt, cur)
    return pltpu.roll(z, LANES - e, 1)


def col_first(dep, base, total_cols):
    off = dep - base - iota(1)
    return jnp.where(off > 0, off - total_cols, off) + HALO


def pack_kernel(first_ref, last_ref, west_ref, east_ref, *, rem, tiles):
    lane = iota(1)
    nf, nl = first_ref.shape[:2]
    for l in range(nl):
        w = jnp.zeros((SUB, LANES), jnp.float32)
        e = jnp.zeros((SUB, LANES), jnp.float32)
        for f in range(nf):
            for rt in range(tiles):
                m = HALO * (f * tiles + rt)
                here = (lane >= m) & (lane < m + HALO)
                a = last_ref[f, l, rt * SUB : rt * SUB + SUB, :]
                b = first_ref[f, l, rt * SUB : rt * SUB + SUB, :]
                w = jnp.where(here, pltpu.roll(a, (m - (rem - HALO)) % LANES, 1), w)
                e = jnp.where(here, pltpu.roll(b, m, 1), e)
        west_ref[l] = w
        east_ref[l] = e


def halo_tiles(west, east, slot, last, rem):
    m = HALO * slot
    prev = pltpu.roll(west, (LANES - HALO - m) % LANES, 1)
    ends = jnp.where(iota(1) < rem, last, pltpu.roll(east, (rem - m) % LANES, 1))
    return prev, ends


def rowpack_kernel(top_ref, bot_ref, west_ref, east_ref, cw_ref, ccw_ref, *, rem, tiles, n, half):
    nf, nl = top_ref.shape[:2]
    band = lax.axis_index("lat")
    sector = lax.axis_index("lon")
    last_band = lax.axis_size("lat") - 1
    sub = iota(0)
    upper = sub < HALO
    full = lambda x: jnp.full((SUB, LANES), x, jnp.int32)
    flip = jnp.where(upper, full(band), last_band - full(band)) == 0
    low = full(sector) < half

    def cut(ref, f, l, q):
        return ref[f, l, :, q * LANES : (q + 1) * LANES] if q < n - 1 else ref[f, l, :, q * LANES :]

    for l in range(nl):
        west, east = west_ref[l], east_ref[l]
        for f in range(nf):
            t = []
            for q in range(n):
                a = top_ref[f, l, :, q * LANES : (q + 1) * LANES]
                b = bot_ref[f, l, :, q * LANES : (q + 1) * LANES]
                t.append(jnp.where(upper, a, b))
            slot_t, slot_b = f * tiles, f * tiles + tiles - 1
            pa, ea = halo_tiles(west, east, slot_t, t[-1], rem)
            pb, eb = halo_tiles(west, east, slot_b, t[-1], rem)
            prev = jnp.where(upper, pa, pb)
            t[-1] = jnp.where(upper, ea, eb)
            for q in range(n):
                v = shifted(t[q - 1] if q else prev, t[q], None, 0)
                r1 = sub % HALO
                rev = jnp.where(
                    r1 == 0,
                    pltpu.roll(v, SUB - 3, 0),
                    jnp.where(
                        r1 == 1,
                        pltpu.roll(v, SUB - 1, 0),
                        jnp.where(r1 == 2, pltpu.roll(v, 1, 0), pltpu.roll(v, 3, 0)),
                    ),
                )
                v = jnp.where(flip, rev, v)
                s = pltpu.roll(v, HALO, 0)
                cw_ref[f, l, :, q * LANES : (q + 1) * LANES] = jnp.where(low, s, v)[:HALO]
                ccw_ref[f, l, :, q * LANES : (q + 1) * LANES] = jnp.where(low, v, s)[:HALO]


def tile_loop(s_ref, base, rt, kr, kc, w, nf, emit):
    r = expand(kr, w[:4])
    c = expand(kc, w[4:])
    for f in range(nf):
        total = None
        for s in range(TAPS):
            line = None
            for t in range(TAPS):
                term = c[t] * s_ref[base(f), t, pl.ds(rt * SUB + HALO + s, SUB), :]
                line = term if line is None else line + term
            line = r[s] * line
            total = line if total is None else total + line
        emit(f, total)


def clear_margins(s_ref, rows):
    zero = jnp.zeros((SUB, LANES), jnp.float32)
    for i in range(s_ref.shape[0]):
        for t in range(TAPS):
            s_ref[i, t, 0:SUB, :] = zero
            s_ref[i, t, SUB + rows : 2 * SUB + rows, :] = zero


def inner_kernel(x_ref, row_ref, col_ref, w_ref, o_ref, s_ref, *, rows, cols, total_cols):
    nf = x_ref.shape[0]
    tiles = rows // SUB
    row0 = lax.axis_index("lat") * rows
    col0 = lax.axis_index("lon") * cols + LANES

    @pl.when(pl.program_id(0) == 0)
    def _():
        clear_margins(s_ref, rows)

    for f in range(nf):
        for rt in range(tiles):
            x = [x_ref[f, 0, rt * SUB : rt * SUB + SUB, q * LANES : (q + 1) * LANES] for q in (0, 1, 2)]
            for t in range(TAPS):
                s_ref[f, t, SUB + rt * SUB : 2 * SUB + rt * SUB, :] = shifted(x[0], x[1], x[2], t)

    def step(rt, carry):
        at = pl.ds(pl.multiple_of(rt * SUB, SUB), SUB)
        kr = row_ref[0, at, :] - (row0 + rt * SUB - HALO) - iota(0)
        kc = col_first(col_ref[0, at, :], col0, total_cols)
        w = [w_ref[b, 0, at, :] for b in range(8)]

        def emit(f, v):
            o_ref[f, 0, at, :] = v

        tile_loop(s_ref, lambda f: f, rt, kr, kc, w, nf, emit)
        return carry

    lax.fori_loop(0, tiles, step, 0)


def outer_kernel(
    x_ref, row_ref, col_ref, w_ref, west_ref, east_ref, mid_ref, o_ref, s_ref, *, rows, cols, rem, n, total_cols
):
    nf = x_ref.shape[0]
    tiles = rows // SUB
    row0 = lax.axis_index("lat") * rows
    col0 = lax.axis_index("lon") * cols

    @pl.when(pl.program_id(0) == 0)
    def _():
        clear_margins(s_ref, rows)

    west, east = west_ref[0], east_ref[0]
    for f in range(nf):
        for rt in range(tiles):
            x = [x_ref[f, 0, rt * SUB : rt * SUB + SUB, q * LANES : (q + 1) * LANES] for q in range(n)]
            prev, x[-1] = halo_tiles(west, east, f * tiles + rt, x[-1], rem)
            to = slice(SUB + rt * SUB, 2 * SUB + rt * SUB)
            for t in range(TAPS):
                s_ref[f, t, to, :] = shifted(prev, x[0], x[1], t)
                s_ref[nf + f, t, to, :] = shifted(x[-2], x[-1], None, t)

    for f in range(nf):
        o_ref[f, 0, :, LANES : 2 * LANES] = mid_ref[f, 0]

    def step(rt, carry):
        at = pl.ds(pl.multiple_of(rt * SUB, SUB), SUB)
        for side, q in enumerate((0, n - 1)):
            lanes = slice(q * LANES, (q + 1) * LANES)
            kr = row_ref[0, at, lanes] - (row0 + rt * SUB - HALO) - iota(0)
            kc = col_first(col_ref[0, at, lanes], col0 + q * LANES, total_cols)
            w = [w_ref[b, 0, at, lanes] for b in range(8)]

            def emit(f, v):
                o_ref[f, 0, at, lanes] = v

            tile_loop(s_ref, lambda f: side * nf + f, rt, kr, kc, w, nf, emit)
        return carry

    lax.fori_loop(0, tiles, step, 0)


def edge_kernel(
    cw_ref, ccw_ref, rt_ref, rb_ref, ct_ref, cb_ref, wt_ref, wb_ref, o_in, o_out, top, bot, sems,
    *, rows, cols, n, half, total_cols
):
    nf, nl = cw_ref.shape[:2]
    ins = [
        pltpu.make_async_copy(o_in.at[:, :, pl.ds(0, SUB), :], top, sems.at[0]),
        pltpu.make_async_copy(o_in.at[:, :, pl.ds(rows - SUB, SUB), :], bot, sems.at[1]),
    ]
    for c in ins:
        c.start()
    for c in ins:
        c.wait()
    row0 = lax.axis_index("lat") * rows
    col0 = lax.axis_index("lon") * cols
    upper = iota(0) < HALO
    low = jnp.full((SUB, LANES), lax.axis_index("lon"), jnp.int32) < half
    lane, sub = iota(1), iota(0)
    zero = jnp.zeros((SUB, LANES), jnp.float32)
    pad = jnp.zeros((SUB - HALO, LANES), jnp.float32)

    def level(l, carry):
        rc = []
        for q in range(n):
            lanes = slice(q * LANES, (q + 1) * LANES)
            pick = lambda a, b: jnp.where(upper, a, b)
            first = pick(sub + row0, sub + (row0 + rows - SUB))
            kr = pick(rt_ref[l, :, lanes], rb_ref[l, :, lanes]) - first + HALO
            kc = col_first(pick(ct_ref[l, :, lanes], cb_ref[l, :, lanes]), col0 + q * LANES, total_cols)
            w = [pick(wt_ref[b, l, :, lanes], wb_ref[b, l, :, lanes]) for b in range(8)]
            r = expand(kr, w[:4])
            rc.append(([pick(r[s], r[s + HALO]) for s in range(HALO)], expand(kc, w[4:])))
        for f in range(nf):
            v = []
            for q in range(n):
                lanes = slice(q * LANES, (q + 1) * LANES)
                a = jnp.concatenate([cw_ref[f, l, :, lanes], pad], axis=0)
                b = jnp.concatenate([ccw_ref[f, l, :, lanes], pad], axis=0)
                a, b = jnp.where(low, a, b), jnp.where(low, b, a)
                v.append([a] + [pltpu.roll(jnp.where(sub < s, b, a), SUB - s, 0) for s in range(1, HALO)])
            v.append([zero] * HALO)
            for q in range(n):
                r, c = rc[q]
                total = None
                for s in range(HALO):
                    line = None
                    for t in range(TAPS):
                        x = v[q][s]
                        if t:
                            x = pltpu.roll(jnp.where(lane < t, v[q + 1][s], x), LANES - t, 1)
                        line = c[t] * x if line is None else line + c[t] * x
                    line = r[s] * line
                    total = line if total is None else total + line
                lanes = slice(q * LANES, min((q + 1) * LANES, cols))
                total = total[:, : min(LANES, cols - q * LANES)]
                keep = upper[:, : total.shape[1]]
                top[f, l, :, lanes] += jnp.where(keep, total, 0.0)
                bot[f, l, :, lanes] += jnp.where(keep, 0.0, total)
        return carry

    lax.fori_loop(0, nl, level, 0)
    outs = [
        pltpu.make_async_copy(top, o_out.at[:, :, pl.ds(0, SUB), :], sems.at[0]),
        pltpu.make_async_copy(bot, o_out.at[:, :, pl.ds(rows - SUB, SUB), :], sems.at[1]),
    ]
    for c in outs:
        c.start()
    for c in outs:
        c.wait()


def circle(lat, lon):
    half = lon // 2
    pairs = []
    for s in range(lon):
        for b in range(lat):
            step = 1 if s < half else -1
            to = (b + step, s) if 0 <= b + step < lat else (b, (s + half) % lon)
            pairs.append((b * lon + s, to[0] * lon + to[1]))
    return pairs


def body(fields, dep_row, dep_col, weights):
    nf, nl, rows, cols = fields.shape
    lat, lon = lax.axis_size("lat"), lax.axis_size("lon")
    n = -(-cols // LANES)
    rem = cols - (n - 1) * LANES
    tiles = rows // SUB
    wide = n * LANES
    half = lon // 2
    total_cols = cols * lon
    assert n == 3 and HALO <= rem <= LANES - HALO and rows % SUB == 0
    f32 = jnp.float32
    shape = jax.ShapeDtypeStruct
    params = lambda: pltpu.CompilerParams(vmem_limit_bytes=VMEM)
    strip = shape((nl, SUB, LANES), f32)
    i0 = lambda *_: (0, 0, 0)

    def lane_block(q):
        return pl.BlockSpec((nf, nl, rows, LANES), lambda i: (0, 0, 0, q))

    west_out, east_out = pl.pallas_call(
        lambda *a: pack_kernel(*a, rem=rem, tiles=tiles),
        grid=(1,),
        in_specs=[lane_block(0), lane_block(n - 1)],
        out_specs=[pl.BlockSpec(strip.shape, i0)] * 2,
        out_shape=[strip, strip],
        compiler_params=params(),
        name="pack",
    )(fields, fields)
    up = [(i, (i + 1) % lon) for i in range(lon)]
    west = lax.ppermute(west_out, "lon", up)
    east = lax.ppermute(east_out, "lon", [(j, i) for i, j in up])

    level4 = lambda k, w: pl.BlockSpec((k, 1, rows, w), lambda l: (0, l, 0, 0))
    level3 = pl.BlockSpec((1, rows, wide), lambda l: (l, 0, 0))
    mid4 = lambda k: pl.BlockSpec((k, 1, rows, LANES), lambda l: (0, l, 0, 1))
    mid3 = pl.BlockSpec((1, rows, LANES), lambda l: (l, 0, 1))
    mid = pl.pallas_call(
        lambda *a: inner_kernel(*a, rows=rows, cols=cols, total_cols=total_cols),
        grid=(nl,),
        in_specs=[level4(nf, wide), mid3, mid3, mid4(8)],
        out_specs=pl.BlockSpec((nf, 1, rows, LANES), lambda l: (0, l, 0, 0)),
        out_shape=shape((nf, nl, rows, LANES), f32),
        scratch_shapes=[pltpu.VMEM((nf, TAPS, rows + 2 * SUB, LANES), f32)],
        compiler_params=params(),
        name="inner",
    )(fields, dep_row, dep_col, weights)

    edge4 = lambda k, r: pl.BlockSpec((k, nl, SUB, wide), lambda i: (0, 0, r, 0))
    edge3 = lambda r: pl.BlockSpec((nl, SUB, wide), lambda i: (0, r, 0))
    band_edge = shape((nf, nl, HALO, wide), f32)
    whole4 = pl.BlockSpec(band_edge.shape, lambda i: (0, 0, 0, 0))
    whole3 = pl.BlockSpec(strip.shape, i0)
    cw, ccw = pl.pallas_call(
        lambda *a: rowpack_kernel(*a, rem=rem, tiles=tiles, n=n, half=half),
        grid=(1,),
        in_specs=[edge4(nf, 0), edge4(nf, tiles - 1), whole3, whole3],
        out_specs=[whole4] * 2,
        out_shape=[band_edge] * 2,
        compiler_params=params(),
        name="rowpack",
    )(fields, fields, west, east)
    ring = circle(lat, lon)
    cw = lax.ppermute(cw, ("lat", "lon"), ring)
    ccw = lax.ppermute(ccw, ("lat", "lon"), [(j, i) for i, j in ring])

    strip_l = pl.BlockSpec((1, SUB, LANES), lambda l: (l, 0, 0))
    out = pl.pallas_call(
        lambda *a: outer_kernel(*a, rows=rows, cols=cols, rem=rem, n=n, total_cols=total_cols),
        grid=(nl,),
        in_specs=[level4(nf, wide), level3, level3, level4(8, wide), strip_l, strip_l,
                  pl.BlockSpec((nf, 1, rows, LANES), lambda l: (0, l, 0, 0))],
        out_specs=level4(nf, wide),
        out_shape=shape(fields.shape, f32),
        scratch_shapes=[pltpu.VMEM((2 * nf, TAPS, rows + 2 * SUB, LANES), f32)],
        compiler_params=params(),
        name="outer",
    )(fields, dep_row, dep_col, weights, west, east, mid)

    hbm = pl.BlockSpec(memory_space=pl.ANY)
    return pl.pallas_call(
        lambda *a: edge_kernel(*a, rows=rows, cols=cols, n=n, half=half, total_cols=total_cols),
        grid=(1,),
        in_specs=[whole4, whole4, edge3(0), edge3(tiles - 1), edge3(0), edge3(tiles - 1),
                  edge4(8, 0), edge4(8, tiles - 1), hbm],
        out_specs=hbm,
        out_shape=shape(fields.shape, f32),
        scratch_shapes=[pltpu.VMEM((nf, nl, SUB, cols), f32), pltpu.VMEM((nf, nl, SUB, cols), f32),
                        pltpu.SemaphoreType.DMA((2,))],
        input_output_aliases={8: 0},
        compiler_params=params(),
        name="edge",
    )(cw, ccw, dep_row, dep_row, dep_col, dep_col, weights, weights, out)


def solution(mesh):
    return jax.shard_map(
        body,
        mesh=mesh,
        in_specs=(
            P(None, None, "lat", "lon"),
            P(None, "lat", "lon"),
            P(None, "lat", "lon"),
            P(None, None, "lat", "lon"),
        ),
        out_specs=P(None, None, "lat", "lon"),
        check_vma=False,
    )
```

time: 63.4 us -> 31.4 us (0.50)
  the two profiles are of different devices: /device:TPU:3 before, /device:TPU:0 now
where the time goes in v1:
time: 31.4 us; the launch traced here: 31.2 us
  Pallas kernels  19.7 us (63%)
  starting transfers between devices  8.18 us (26%)
  waiting for transfers between devices  1.99 us (6%)
  local copies, waits for them, and re-layouts  1.28 us (4%)
    pallas_call x1, Pallas kernels, body(): pl.pallas_call(lambda *a: outer_kernel(*a, rows=rows, cols=cols, rem=rem,...  10.8 us
    pallas_call x1, Pallas kernels, body(): pl.pallas_call(lambda *a: edge_kernel(*a, rows=rows, cols=cols, n=n, half...  4.5 us
    pallas_call x1, Pallas kernels, body(): pl.pallas_call(lambda *a: inner_kernel(*a, rows=rows, cols=cols, total_co...  3.66 us
    ppermute x1, starting transfers between devices, body(): west = lax.ppermute(west_out, 'lon', up)  3.1 us
    ppermute x1, starting transfers between devices, body(): ccw = lax.ppermute(ccw, ('lat', 'lon'), [(j, i) for i, j in ring])  2.91 us
    ppermute x1, starting transfers between devices, body(): east = lax.ppermute(east_out, 'lon', [(j, i) for i, j in up])  2.1 us
    ppermute x1, waiting for transfers between devices, body(): west = lax.ppermute(west_out, 'lon', up)  1.83 us
    unnamed x8, local copies, waits for them, and re-layouts  1.28 us
  transfers between devices with their start and end apart: 4, of which 2 were waited for; matrix products, arithmetic and copies ran while one was open for 0% of the time, Pallas kernels for 46%

profile of v1, /device:TPU:0, one launch (start us, length us, event | category | flops | bytes accessed | tf_op | source)
XLA Modules:
  0.0 31.2 jit_solution(2158580078074606259)
XLA Ops:
  0.0 0.0 copy-start
  0.0 1.3 %copy-done = f32[4,6,32,320]{3,2,1,0:T(8,128)S(1)} copy-done((f32[4,6,32,320]{3,2,1,0:T(8,128)S(1)}, f32[4,6,32,320]{3,2,1,0:T(8,128)}, u32[]{:S(2)}) %copy-start) | copy-done | bytes 983064
  1.3 0.0 copy-start.2
  1.3 0.0 copy-start.3
  1.3 0.3 pack.1
  1.5 3.1 %collective-permute-start = (f32[6,8,128]{2,1,0:T(8,128)S(1)}, f32[6,8,128]{2,1,0:T(8,128)S(1)}, u32[]{:S(2)}, u32[]{:S(2)}) collective-permute-start(f32[6,8,128]{2,1,0:T(8,128)S(1)} %get-tuple-element.9), channel_id=1, source_target_pairs={{0,1},{1,2},{2,3},{3,0},{4,5},{5,6},{6,7},{7,4},{8,9},{9,10},{10,1... | collective-permute-start | bytes 73736 | tf_op jit(solution)/shard_map/ppermute | solution.py:325
  4.6 0.0 copy-start.1
  4.6 2.1 %collective-permute-start.1 = (f32[6,8,128]{2,1,0:T(8,128)S(1)}, f32[6,8,128]{2,1,0:T(8,128)S(1)}, u32[]{:S(2)}, u32[]{:S(2)}) collective-permute-start(f32[6,8,128]{2,1,0:T(8,128)S(1)} %get-tuple-element.10), channel_id=1, source_target_pairs={{1,0},{2,1},{3,2},{0,3},{5,4},{6,5},{7,6},{4,7},{9,8},{10,9},{11,1... | collective-permute-start | bytes 73736 | tf_op jit(solution)/shard_map/ppermute | solution.py:326
  6.7 1.8 %collective-permute-done.a_2_.a_4_ = f32[6,8,128]{2,1,0:T(8,128)S(1)} collective-permute-done((f32[6,8,128]{2,1,0:T(8,128)S(1)}, f32[6,8,128]{2,1,0:T(8,128)S(1)}, u32[]{:S(2)}, u32[]{:S(2)}) %collective-permute-start) | collective-permute-done | bytes 24608 | tf_op jit(solution)/shard_map/ppermute | solution.py:325
  8.6 0.2 collective-permute-done.1.a_3_.a_5_
  8.7 0.6 %rowpack.1 = (f32[4,6,4,384]{3,2,1,0:T(4,128)S(1)}, f32[4,6,4,384]{3,2,1,0:T(4,128)S(1)}) custom-call(f32[4,6,32,320]{3,2,1,0:T(8,128)S(1)} %copy-done, f32[4,6,32,320]{3,2,1,0:T(8,128)S(1)} %copy-done, f32[6,8,128]{2,1,0:T(8,128)S(1)} %collective-permute-done.a_2_.a_4_, f32[6,8,128]{2,1,0:T(8,128)S(1)} %collective-permute-done.1.a_3_.a_5_), custom_call_target="tpu_custom_call" | custom-call | tf_op jit(solution)/shard_map/rowpack/pallas_call | solution.py:348
  9.3 0.1 collective-permute-start.2
  9.4 2.9 %collective-permute-start.3 = (f32[4,6,4,384]{3,2,1,0:T(4,128)S(1)}, f32[4,6,4,384]{3,2,1,0:T(4,128)S(1)}, u32[]{:S(2)}, u32[]{:S(2)}) collective-permute-start(f32[4,6,4,384]{3,2,1,0:T(4,128)S(1)} %get-tuple-element.12), channel_id=1, source_target_pairs={{4,0},{8,4},{12,8},{16,12},{20,16},{24,20},{28,24},{30,28},{5,1},{... | collective-permute-start | bytes 442376 | tf_op jit(solution)/shard_map/ppermute | solution.py:359
  12.3 0.0 copy-done.2
  12.3 0.0 copy-done.3
  12.3 0.0 copy-done.1
  12.3 3.7 %inner.1.a_6_ = f32[4,6,32,128]{3,2,1,0:T(8,128)S(1)} custom-call(f32[4,6,32,320]{3,2,1,0:T(8,128)S(1)} %copy-done, s32[6,32,320]{2,1,0:T(8,128)S(1)} %copy-done.2, s32[6,32,320]{2,1,0:T(8,128)S(1)} %copy-done.3, f32[8,6,32,320]{3,2,1,0:T(8,128)S(1)} %copy-done.1), custom_call_target="tpu_custom_call" | custom-call | tf_op jit(solution)/shard_map/inner/pallas_call | solution.py:332
  16.0 10.8 %outer.1.a_8_ = f32[4,6,32,320]{3,2,1,0:T(8,128)} custom-call(f32[4,6,32,320]{3,2,1,0:T(8,128)S(1)} %copy-done, s32[6,32,320]{2,1,0:T(8,128)S(1)} %copy-done.2, s32[6,32,320]{2,1,0:T(8,128)S(1)} %copy-done.3, f32[8,6,32,320]{3,2,1,0:T(8,128)S(1)} %copy-done.1, f32[6,8,128]{2,1,0:T(8,128)S(1)} %collective-permute-done.a_2_.a_4_, ...), custom_call_target="tpu_custom_call" | custom-call | tf_op jit(solution)/shard_map/outer/pallas_call | solution.py:362
  26.7 0.0 collective-permute-done.2.a_0_
  26.7 0.0 collective-permute-done.3.a_1_
  26.7 4.5 %edge.1 = f32[4,6,32,320]{3,2,1,0:T(8,128)} custom-call(f32[4,6,4,384]{3,2,1,0:T(4,128)S(1)} %collective-permute-done.2.a_0_, f32[4,6,4,384]{3,2,1,0:T(4,128)S(1)} %collective-permute-done.3.a_1_, s32[6,32,320]{2,1,0:T(8,128)S(1)} %copy-done.2, s32[6,32,320]{2,1,0:T(8,128)S(1)} %copy-done.2, ...), custom_call_target="tpu_custom_call", output_to_operand_aliasing={{}: (8, {})} | custom-call | tf_op jit(solution)/shard_map/edge/pallas_call | solution.py:375
Async XLA Ops:
  0.0 1.3 %copy-start = (f32[4,6,32,320]{3,2,1,0:T(8,128)S(1)}, f32[4,6,32,320]{3,2,1,0:T(8,128)}, u32[]{:S(2)}) copy-start(f32[4,6,32,320]{3,2,1,0:T(8,128)} %a_0_.7) | copy-start | bytes 2949124
  1.3 11.0 %copy-start.2 = (s32[6,32,320]{2,1,0:T(8,128)S(1)}, s32[6,32,320]{2,1,0:T(8,128)}, u32[]{:S(2)}) copy-start(s32[6,32,320]{2,1,0:T(8,128)} %a_3_.5) | copy-start | bytes 737284
  1.3 11.0 %copy-start.3 = (s32[6,32,320]{2,1,0:T(8,128)S(1)}, s32[6,32,320]{2,1,0:T(8,128)}, u32[]{:S(2)}) copy-start(s32[6,32,320]{2,1,0:T(8,128)} %a_5_.1) | copy-start | bytes 737284
  1.5 7.0 %collective-permute-start = (f32[6,8,128]{2,1,0:T(8,128)S(1)}, f32[6,8,128]{2,1,0:T(8,128)S(1)}, u32[]{:S(2)}, u32[]{:S(2)}) collective-permute-start(f32[6,8,128]{2,1,0:T(8,128)S(1)} %get-tuple-element.9), channel_id=1, source_target_pairs={{0,1},{1,2},{2,3},{3,0},{4,5},{5,6},{6,7},{7,4},{8,9},{9,10},{10,1... | collective-permute-start | bytes 73736 | tf_op jit(solution)/shard_map/ppermute | solution.py:325
  4.6 7.7 %copy-start.1 = (f32[8,6,32,320]{3,2,1,0:T(8,128)S(1)}, f32[8,6,32,320]{3,2,1,0:T(8,128)}, u32[]{:S(2)}) copy-start(f32[8,6,32,320]{3,2,1,0:T(8,128)} %a_7_.1) | copy-start | bytes 5898244
  4.6 4.1 %collective-permute-start.1 = (f32[6,8,128]{2,1,0:T(8,128)S(1)}, f32[6,8,128]{2,1,0:T(8,128)S(1)}, u32[]{:S(2)}, u32[]{:S(2)}) collective-permute-start(f32[6,8,128]{2,1,0:T(8,128)S(1)} %get-tuple-element.10), channel_id=1, source_target_pairs={{1,0},{2,1},{3,2},{0,3},{5,4},{6,5},{7,6},{4,7},{9,8},{10,9},{11,1... | collective-permute-start | bytes 73736 | tf_op jit(solution)/shard_map/ppermute | solution.py:326
  9.3 17.4 %collective-permute-start.2 = (f32[4,6,4,384]{3,2,1,0:T(4,128)S(1)}, f32[4,6,4,384]{3,2,1,0:T(4,128)S(1)}, u32[]{:S(2)}, u32[]{:S(2)}) collective-permute-start(f32[4,6,4,384]{3,2,1,0:T(4,128)S(1)} %get-tuple-element.11), channel_id=1, source_target_pairs={{0,4},{4,8},{8,12},{12,16},{16,20},{20,24},{24,28},{28,30},{1,5},{... | collective-permute-start | bytes 442376 | tf_op jit(solution)/shard_map/ppermute | solution.py:358
  9.4 17.4 %collective-permute-start.3 = (f32[4,6,4,384]{3,2,1,0:T(4,128)S(1)}, f32[4,6,4,384]{3,2,1,0:T(4,128)S(1)}, u32[]{:S(2)}, u32[]{:S(2)}) collective-permute-start(f32[4,6,4,384]{3,2,1,0:T(4,128)S(1)} %get-tuple-element.12), channel_id=1, source_target_pairs={{4,0},{8,4},{12,8},{16,12},{20,16},{24,20},{28,24},{30,28},{5,1},{... | collective-permute-start | bytes 442376 | tf_op jit(solution)/shard_map/ppermute | solution.py:359

commit v2 on v1

v2 whole, which is shorter than its diff:
```python
import jax
import jax.numpy as jnp
from jax import lax
from jax.experimental import pallas as pl
from jax.experimental.pallas import tpu as pltpu
from jax.sharding import PartitionSpec as P

HALO = 4
TAPS = 2 * HALO
LANES = 128
SUB = 8
VMEM = 24 * 1024 * 1024


def iota(dim):
    return lax.broadcasted_iota(jnp.int32, (SUB, LANES), dim)


def tile(ref, lead, row, q, n, rem):
    at = pl.ds(row, SUB)
    if q < n - 1 or rem == LANES:
        return ref[(*lead, at, slice(q * LANES, (q + 1) * LANES))]
    part = ref[(*lead, at, slice(q * LANES, q * LANES + rem))]
    fill = jnp.zeros((SUB, LANES - rem), part.dtype)
    return jnp.concatenate([part, fill], axis=1)


def expand(k, w):
    masks = [k == v for v in range(HALO + 1)]
    out = []
    for t in range(TAPS):
        val = jnp.zeros((SUB, LANES), jnp.float32)
        for v in range(HALO + 1):
            if 0 <= t - v < 4:
                val = jnp.where(masks[v], w[t - v], val)
        out.append(val)
    return out


def shifted(prev, cur, nxt, t):
    lane = iota(1)
    if t < HALO:
        d = HALO - t
        return pltpu.roll(jnp.where(lane >= LANES - d, prev, cur), d, 1)
    if t == HALO:
        return cur
    e = t - HALO
    z = cur if nxt is None else jnp.where(lane < e, nxt, cur)
    return pltpu.roll(z, LANES - e, 1)


def col_first(dep, base, total_cols):
    off = dep - base - iota(1)
    return jnp.where(off > 0, off - total_cols, off) + HALO


def pack_kernel(x_ref, west_ref, east_ref, *, rem, tiles, n):
    lane = iota(1)
    nf, nl = x_ref.shape[:2]
    for l in range(nl):
        w = jnp.zeros((SUB, LANES), jnp.float32)
        e = jnp.zeros((SUB, LANES), jnp.float32)
        for f in range(nf):
            for rt in range(tiles):
                m = HALO * (f * tiles + rt)
                here = (lane >= m) & (lane < m + HALO)
                a = tile(x_ref, (f, l), rt * SUB, n - 1, n, rem)
                b = tile(x_ref, (f, l), rt * SUB, 0, n, rem)
                w = jnp.where(here, pltpu.roll(a, (m - (rem - HALO)) % LANES, 1), w)
                e = jnp.where(here, pltpu.roll(b, m, 1), e)
        west_ref[l] = w
        east_ref[l] = e


def halo_tiles(west, east, slot, last, rem):
    m = HALO * slot
    prev = pltpu.roll(west, (LANES - HALO - m) % LANES, 1)
    ends = jnp.where(iota(1) < rem, last, pltpu.roll(east, (rem - m) % LANES, 1))
    return prev, ends


def rowpack_kernel(x_ref, west_ref, east_ref, after, cw_ref, ccw_ref, *, rem, tiles, n, half):
    nf, nl, rows, _ = x_ref.shape
    band = lax.axis_index("lat")
    sector = lax.axis_index("lon")
    last_band = lax.axis_size("lat") - 1
    sub = iota(0)
    upper = sub < HALO
    full = lambda x: jnp.full((SUB, LANES), x, jnp.int32)
    flip = jnp.where(upper, full(band), last_band - full(band)) == 0
    low = full(sector) < half

    for l in range(nl):
        west, east = west_ref[l], east_ref[l]
        for f in range(nf):
            t = []
            for q in range(n):
                a = tile(x_ref, (f, l), 0, q, n, rem)
                b = tile(x_ref, (f, l), rows - SUB, q, n, rem)
                t.append(jnp.where(upper, a, b))
            slot_t, slot_b = f * tiles, f * tiles + tiles - 1
            pa, ea = halo_tiles(west, east, slot_t, t[-1], rem)
            pb, eb = halo_tiles(west, east, slot_b, t[-1], rem)
            prev = jnp.where(upper, pa, pb)
            t[-1] = jnp.where(upper, ea, eb)
            for q in range(n):
                v = shifted(t[q - 1] if q else prev, t[q], None, 0)
                r1 = sub % HALO
                rev = jnp.where(
                    r1 == 0,
                    pltpu.roll(v, SUB - 3, 0),
                    jnp.where(
                        r1 == 1,
                        pltpu.roll(v, SUB - 1, 0),
                        jnp.where(r1 == 2, pltpu.roll(v, 1, 0), pltpu.roll(v, 3, 0)),
                    ),
                )
                v = jnp.where(flip, rev, v)
                s = pltpu.roll(v, HALO, 0)
                cw_ref[f, l, :, q * LANES : (q + 1) * LANES] = jnp.where(low, s, v)[:HALO]
                ccw_ref[f, l, :, q * LANES : (q + 1) * LANES] = jnp.where(low, v, s)[:HALO]


def tile_loop(s_ref, base, rt, kr, kc, w, nf, emit):
    r = expand(kr, w[:4])
    c = expand(kc, w[4:])
    for f in range(nf):
        total = None
        for s in range(TAPS):
            line = None
            for t in range(TAPS):
                term = c[t] * s_ref[base(f), t, pl.ds(rt * SUB + HALO + s, SUB), :]
                line = term if line is None else line + term
            line = r[s] * line
            total = line if total is None else total + line
        emit(f, total)


def clear_margins(s_ref, rows):
    zero = jnp.zeros((SUB, LANES), jnp.float32)
    for i in range(s_ref.shape[0]):
        for t in range(TAPS):
            s_ref[i, t, 0:SUB, :] = zero
            s_ref[i, t, SUB + rows : 2 * SUB + rows, :] = zero


def inner_kernel(x_ref, row_ref, col_ref, w_ref, o_ref, s_ref, *, rows, cols, rem, n, total_cols):
    nf, nl = x_ref.shape[:2]
    tiles = rows // SUB
    row0 = lax.axis_index("lat") * rows
    col0 = lax.axis_index("lon") * cols + LANES
    mid = slice(LANES, 2 * LANES)
    clear_margins(s_ref, rows)

    def level(l, carry):
        for f in range(nf):
            for rt in range(tiles):
                x = [tile(x_ref, (f, l), rt * SUB, q, n, rem) for q in range(n)]
                for t in range(TAPS):
                    s_ref[f, t, SUB + rt * SUB : 2 * SUB + rt * SUB, :] = shifted(x[0], x[1], x[2], t)

        def step(rt, carry):
            at = pl.ds(pl.multiple_of(rt * SUB, SUB), SUB)
            kr = row_ref[l, at, mid] - (row0 + rt * SUB - HALO) - iota(0)
            kc = col_first(col_ref[l, at, mid], col0, total_cols)
            w = [w_ref[b, l, at, mid] for b in range(8)]

            def emit(f, v):
                o_ref[f, l, at, :] = v

            tile_loop(s_ref, lambda f: f, rt, kr, kc, w, nf, emit)
            return carry

        return lax.fori_loop(0, tiles, step, carry)

    lax.fori_loop(0, nl, level, 0)


def outer_kernel(
    x_ref, row_ref, col_ref, w_ref, west_ref, east_ref, o_ref, s_ref, *, rows, cols, rem, n, total_cols
):
    nf, nl = x_ref.shape[:2]
    tiles = rows // SUB
    row0 = lax.axis_index("lat") * rows
    col0 = lax.axis_index("lon") * cols
    clear_margins(s_ref, rows)

    def level(l, carry):
        west, east = west_ref[l], east_ref[l]
        for side, q in enumerate((0, n - 1)):
            for f in range(nf):
                for rt in range(tiles):
                    slot = f * tiles + rt
                    prev, nxt = None, None
                    if q:
                        prev = tile(x_ref, (f, l), rt * SUB, n - 2, n, rem)
                        cur = halo_tiles(west, east, slot, tile(x_ref, (f, l), rt * SUB, n - 1, n, rem), rem)[1]
                    else:
                        cur = tile(x_ref, (f, l), rt * SUB, 0, n, rem)
                        nxt = tile(x_ref, (f, l), rt * SUB, 1, n, rem)
                        prev = halo_tiles(west, east, slot, cur, rem)[0]
                    to = slice(SUB + rt * SUB, 2 * SUB + rt * SUB)
                    for t in range(TAPS):
                        s_ref[f, t, to, :] = shifted(prev, cur, nxt, t)

            def step(rt, carry):
                row = pl.multiple_of(rt * SUB, SUB)
                at = pl.ds(row, SUB)
                kr = tile(row_ref, (l,), row, q, n, rem) - (row0 + rt * SUB - HALO) - iota(0)
                kc = col_first(tile(col_ref, (l,), row, q, n, rem), col0 + q * LANES, total_cols)
                w = [tile(w_ref, (b, l), row, q, n, rem) for b in range(8)]

                def emit(f, v):
                    o_ref[f, l, at, side * LANES : (side + 1) * LANES] = v

                tile_loop(s_ref, lambda f: f, rt, kr, kc, w, nf, emit)
                return carry

            lax.fori_loop(0, tiles, step, 0)
        return carry

    lax.fori_loop(0, nl, level, 0)


def edge_kernel(
    cw_ref, ccw_ref, row_ref, col_ref, w_ref, mid_ref, out_ref, o_out, buf, sems,
    *, rows, cols, rem, n, half, total_cols
):
    nf, nl = cw_ref.shape[:2]
    row0 = lax.axis_index("lat") * rows
    col0 = lax.axis_index("lon") * cols
    upper = iota(0) < HALO
    low = jnp.full((SUB, LANES), lax.axis_index("lon"), jnp.int32) < half
    lane, sub = iota(1), iota(0)
    zero = jnp.zeros((SUB, LANES), jnp.float32)
    pad = jnp.zeros((SUB - HALO, LANES), jnp.float32)
    pick = lambda a, b: jnp.where(upper, a, b)
    down = rows - SUB

    def copy(l):
        return pltpu.make_async_copy(buf.at[:, l], o_out.at[:, l], sems.at[l])

    def level(l, carry):
        rc = []
        for q in range(n):
            both = lambda ref, lead: pick(tile(ref, lead, 0, q, n, rem), tile(ref, lead, down, q, n, rem))
            first = pick(sub + row0, sub + (row0 + down))
            kr = both(row_ref, (l,)) - first + HALO
            kc = col_first(both(col_ref, (l,)), col0 + q * LANES, total_cols)
            w = [both(w_ref, (b, l)) for b in range(8)]
            r = expand(kr, w[:4])
            rc.append(([pick(r[s], r[s + HALO]) for s in range(HALO)], expand(kc, w[4:])))
        for f in range(nf):
            v = []
            for q in range(n):
                lanes = slice(q * LANES, (q + 1) * LANES)
                a = jnp.concatenate([cw_ref[f, l, :, lanes], pad], axis=0)
                b = jnp.concatenate([ccw_ref[f, l, :, lanes], pad], axis=0)
                a, b = jnp.where(low, a, b), jnp.where(low, b, a)
                v.append([a] + [pltpu.roll(jnp.where(sub < s, b, a), SUB - s, 0) for s in range(1, HALO)])
            v.append([zero] * HALO)
            for q in range(n):
                r, c = rc[q]
                total = None
                for s in range(HALO):
                    line = None
                    for t in range(TAPS):
                        x = v[q][s]
                        if t:
                            x = pltpu.roll(jnp.where(lane < t, v[q + 1][s], x), LANES - t, 1)
                        line = c[t] * x if line is None else line + c[t] * x
                    line = r[s] * line
                    total = line if total is None else total + line
                width = min(LANES, cols - q * LANES)
                lanes = slice(q * LANES, q * LANES + width)
                for rt in range(rows // SUB):
                    at = slice(rt * SUB, rt * SUB + SUB)
                    if q == 1:
                        val = mid_ref[f, l, at, :]
                    else:
                        side = 1 if q else 0
                        val = out_ref[f, l, at, side * LANES : (side + 1) * LANES]
                    if rt == 0:
                        val = val + jnp.where(upper, total, 0.0)
                    if rt == rows // SUB - 1:
                        val = val + jnp.where(upper, 0.0, total)
                    buf[f, l, at, lanes] = val[:, :width]
        copy(l).start()
        return carry

    lax.fori_loop(0, nl, level, 0)
    for l in range(nl):
        copy(l).wait()


def circle(lat, lon):
    half = lon // 2
    pairs = []
    for s in range(lon):
        for b in range(lat):
            step = 1 if s < half else -1
            to = (b + step, s) if 0 <= b + step < lat else (b, (s + half) % lon)
            pairs.append((b * lon + s, to[0] * lon + to[1]))
    return pairs


def body(fields, dep_row, dep_col, weights):
    nf, nl, rows, cols = fields.shape
    lat, lon = lax.axis_size("lat"), lax.axis_size("lon")
    n = -(-cols // LANES)
    rem = cols - (n - 1) * LANES
    tiles = rows // SUB
    wide = n * LANES
    half = lon // 2
    total_cols = cols * lon
    assert n == 3 and HALO <= rem <= LANES - HALO and rows % SUB == 0
    f32 = jnp.float32
    shape = jax.ShapeDtypeStruct
    params = lambda: pltpu.CompilerParams(vmem_limit_bytes=VMEM)
    strip = shape((nl, SUB, LANES), f32)
    vmem = pl.BlockSpec(memory_space=pltpu.VMEM)
    hbm = pl.BlockSpec(memory_space=pl.ANY)

    west_out, east_out = pl.pallas_call(
        lambda *a: pack_kernel(*a, rem=rem, tiles=tiles, n=n),
        in_specs=[vmem],
        out_specs=[vmem] * 2,
        out_shape=[strip, strip],
        compiler_params=params(),
        name="pack",
    )(fields)
    up = [(i, (i + 1) % lon) for i in range(lon)]
    west = lax.ppermute(west_out, "lon", up)
    east = lax.ppermute(east_out, "lon", [(j, i) for i, j in up])

    mid = pl.pallas_call(
        lambda *a: inner_kernel(*a, rows=rows, cols=cols, rem=rem, n=n, total_cols=total_cols),
        in_specs=[vmem] * 4,
        out_specs=vmem,
        out_shape=shape((nf, nl, rows, LANES), f32),
        scratch_shapes=[pltpu.VMEM((nf, TAPS, rows + 2 * SUB, LANES), f32)],
        compiler_params=params(),
        name="inner",
    )(fields, dep_row, dep_col, weights)

    band_edge = shape((nf, nl, HALO, wide), f32)
    cw, ccw = pl.pallas_call(
        lambda *a: rowpack_kernel(*a, rem=rem, tiles=tiles, n=n, half=half),
        in_specs=[vmem] * 3 + [hbm],
        out_specs=[vmem] * 2,
        out_shape=[band_edge] * 2,
        compiler_params=params(),
        name="rowpack",
    )(fields, west, east, mid)
    ring = circle(lat, lon)
    cw = lax.ppermute(cw, ("lat", "lon"), ring)
    ccw = lax.ppermute(ccw, ("lat", "lon"), [(j, i) for i, j in ring])

    out = pl.pallas_call(
        lambda *a: outer_kernel(*a, rows=rows, cols=cols, rem=rem, n=n, total_cols=total_cols),
        in_specs=[vmem] * 6,
        out_specs=vmem,
        out_shape=shape((nf, nl, rows, 2 * LANES), f32),
        scratch_shapes=[pltpu.VMEM((nf, TAPS, rows + 2 * SUB, LANES), f32)],
        compiler_params=params(),
        name="outer",
    )(fields, dep_row, dep_col, weights, west, east)

    return pl.pallas_call(
        lambda *a: edge_kernel(*a, rows=rows, cols=cols, rem=rem, n=n, half=half, total_cols=total_cols),
        in_specs=[vmem] * 7,
        out_specs=hbm,
        out_shape=shape(fields.shape, f32),
        scratch_shapes=[pltpu.VMEM(fields.shape, f32), pltpu.SemaphoreType.DMA((nl,))],
        compiler_params=params(),
        name="edge",
    )(cw, ccw, dep_row, dep_col, weights, mid, out)


def solution(mesh):
    return jax.shard_map(
        body,
        mesh=mesh,
        in_specs=(
            P(None, None, "lat", "lon"),
            P(None, "lat", "lon"),
            P(None, "lat", "lon"),
            P(None, None, "lat", "lon"),
        ),
        out_specs=P(None, None, "lat", "lon"),
        check_vma=False,
    )
```

time: 31.4 us -> 26.2 us (0.83)
  Pallas kernels: 19.7 us -> 14.8 us
  waiting for transfers between devices: 1.99 us -> 0.01 us
  local copies, waits for them, and re-layouts: 1.28 us -> 2.95 us
    pallas_call x1, Pallas kernels: 10.8 us -> 7.39 us  [body(): pl.pallas_call(lambda *a: outer_kernel(*a, rows=rows, cols=cols, rem=rem,...]
    ppermute x1, waiting for transfers between devices: 1.83 us -> 0.01 us  [body(): west = lax.ppermute(west_out, 'lon', up)]
    unnamed x8 -> x10, local copies, waits for them, and re-layouts: 1.28 us -> 2.95 us
    pallas_call x3, Pallas kernels: 8.41 us -> 6.88 us  [the longest x1 3.33 us: body(): pl.pallas_call(lambda *a: edge_kernel(*a, rows=rows, cols=cols, rem=rem,...]
  transfers between devices with their start and end apart: 4 -> 4, of which waited for: 2 -> 0; matrix products, arithmetic and copies ran while one was open for 0% -> 0% of each run, Pallas kernels for 46% -> 41%
where the time goes in v2:
time: 26.2 us; the launch traced here: 26 us
  Pallas kernels  14.8 us (56%)
  starting transfers between devices  8.17 us (31%)
  local copies, waits for them, and re-layouts  2.95 us (11%)
    pallas_call x1, Pallas kernels, body(): pl.pallas_call(lambda *a: outer_kernel(*a, rows=rows, cols=cols, rem=rem,...  7.39 us
    pallas_call x1, Pallas kernels, body(): pl.pallas_call(lambda *a: edge_kernel(*a, rows=rows, cols=cols, rem=rem,...  3.33 us
    pallas_call x1, Pallas kernels, body(): pl.pallas_call(lambda *a: inner_kernel(*a, rows=rows, cols=cols, rem=rem,...  3.3 us
    ppermute x1, starting transfers between devices, body(): west = lax.ppermute(west_out, 'lon', up)  3.1 us
    unnamed x10, local copies, waits for them, and re-layouts  2.95 us
    ppermute x1, starting transfers between devices, body(): ccw = lax.ppermute(ccw, ('lat', 'lon'), [(j, i) for i, j in ring])  2.91 us
    ppermute x1, starting transfers between devices, body(): east = lax.ppermute(east_out, 'lon', [(j, i) for i, j in up])  2.09 us
    pallas_call x1, Pallas kernels, body(): pl.pallas_call(lambda *a: rowpack_kernel(*a, rem=rem, tiles=tiles, n=n, h...  0.56 us
  transfers between devices with their start and end apart: 4, of which 0 were waited for; matrix products, arithmetic and copies ran while one was open for 0% of the time, Pallas kernels for 41%

profile of v2, /device:TPU:0, one launch (start us, length us, event | category | flops | bytes accessed | tf_op | source)
XLA Modules:
  0.0 26.0 jit_solution(13697554488815738495)
XLA Ops:
  0.0 0.0 copy-start.2
  0.0 1.3 %copy-done.2 = f32[4,6,32,320]{3,2,1,0:T(8,128)S(1)} copy-done((f32[4,6,32,320]{3,2,1,0:T(8,128)S(1)}, f32[4,6,32,320]{3,2,1,0:T(8,128)}, u32[]{:S(2)}) %copy-start.2) | copy-done | bytes 983064
  1.3 0.0 copy-start.3
  1.3 0.0 copy-start.4
  1.3 0.3 pack.1
  1.5 3.1 %collective-permute-start = (f32[6,8,128]{2,1,0:T(8,128)S(1)}, f32[6,8,128]{2,1,0:T(8,128)S(1)}, u32[]{:S(2)}, u32[]{:S(2)}) collective-permute-start(f32[6,8,128]{2,1,0:T(8,128)S(1)} %get-tuple-element.9), channel_id=1, source_target_pairs={{0,1},{1,2},{2,3},{3,0},{4,5},{5,6},{6,7},{7,4},{8,9},{9,10},{10,1... | collective-permute-start | bytes 73736 | tf_op jit(solution)/shard_map/ppermute | solution.py:333
  4.6 2.1 %collective-permute-start.1 = (f32[6,8,128]{2,1,0:T(8,128)S(1)}, f32[6,8,128]{2,1,0:T(8,128)S(1)}, u32[]{:S(2)}, u32[]{:S(2)}) collective-permute-start(f32[6,8,128]{2,1,0:T(8,128)S(1)} %get-tuple-element.10), channel_id=1, source_target_pairs={{1,0},{2,1},{3,2},{0,3},{5,4},{6,5},{7,6},{4,7},{9,8},{10,9},{11,1... | collective-permute-start | bytes 73736 | tf_op jit(solution)/shard_map/ppermute | solution.py:334
  6.7 0.0 copy-done.3
  6.7 0.0 copy-done.4
  6.7 0.0 copy-start
  6.7 1.7 %copy-done = f32[8,6,32,320]{3,2,1,0:T(8,128)S(1)} copy-done((f32[8,6,32,320]{3,2,1,0:T(8,128)S(1)}, f32[8,6,32,320]{3,2,1,0:T(8,128)}, u32[]{:S(2)}) %copy-start) | copy-done | bytes 1966104
  8.4 0.0 copy-start.1
  8.4 3.3 %inner.1.a_3_.a_5_ = f32[4,6,32,128]{3,2,1,0:T(8,128)S(1)} custom-call(f32[4,6,32,320]{3,2,1,0:T(8,128)S(1)} %copy-done.2, s32[6,32,320]{2,1,0:T(8,128)S(1)} %copy-done.3, s32[6,32,320]{2,1,0:T(8,128)S(1)} %copy-done.4, f32[8,6,32,320]{3,2,1,0:T(8,128)S(1)} %copy-done), custom_call_target="tpu_custom_call" | custom-call | tf_op jit(solution)/shard_map/inner/pallas_call | solution.py:336
  11.7 0.0 collective-permute-done.a_1_.a_4_
  11.7 0.0 collective-permute-done.1.a_2_.a_5_
  11.7 0.6 %rowpack.1 = (f32[4,6,4,384]{3,2,1,0:T(4,128)S(1)}, f32[4,6,4,384]{3,2,1,0:T(4,128)S(1)}) custom-call(f32[4,6,32,320]{3,2,1,0:T(8,128)S(1)} %copy-done.2, f32[6,8,128]{2,1,0:T(8,128)S(1)} %collective-permute-done.a_1_.a_4_, f32[6,8,128]{2,1,0:T(8,128)S(1)} %collective-permute-done.1.a_2_.a_5_, f32[4,6,32,128]{3,2,1,0:T(8,128)S(1)} %inner.1.a_3_.a_5_), custom_call_target="tpu_custom_call" | custom-call | tf_op jit(solution)/shard_map/rowpack/pallas_call | solution.py:347
  12.3 0.1 collective-permute-start.2
  12.4 2.9 %collective-permute-start.3 = (f32[4,6,4,384]{3,2,1,0:T(4,128)S(1)}, f32[4,6,4,384]{3,2,1,0:T(4,128)S(1)}, u32[]{:S(2)}, u32[]{:S(2)}) collective-permute-start(f32[4,6,4,384]{3,2,1,0:T(4,128)S(1)} %get-tuple-element.12), channel_id=1, source_target_pairs={{4,0},{8,4},{12,8},{16,12},{20,16},{24,20},{28,24},{30,28},{5,1},{... | collective-permute-start | bytes 442376 | tf_op jit(solution)/shard_map/ppermute | solution.py:357
  15.3 0.0 copy-done.1
  15.3 7.4 %outer.1.a_6_ = f32[4,6,32,256]{3,2,1,0:T(8,128)S(1)} custom-call(f32[4,6,32,320]{3,2,1,0:T(8,128)S(1)} %copy-done.2, s32[6,32,320]{2,1,0:T(8,128)S(1)} %copy-done.3, s32[6,32,320]{2,1,0:T(8,128)S(1)} %copy-done.4, f32[8,6,32,320]{3,2,1,0:T(8,128)S(1)} %copy-done.1, f32[6,8,128]{2,1,0:T(8,128)S(1)} %collective-permute-done.a_1_.a_4_, ...), custom_call_target="tpu_custom_call" | custom-call | tf_op jit(solution)/shard_map/outer/pallas_call | solution.py:359
  22.7 0.0 collective-permute-done.2.a_0_
  22.7 0.0 collective-permute-done.3.a_1_
  22.7 3.3 %edge.1 = f32[4,6,32,320]{3,2,1,0:T(8,128)} custom-call(f32[4,6,4,384]{3,2,1,0:T(4,128)S(1)} %collective-permute-done.2.a_0_, f32[4,6,4,384]{3,2,1,0:T(4,128)S(1)} %collective-permute-done.3.a_1_, s32[6,32,320]{2,1,0:T(8,128)S(1)} %copy-done.3, s32[6,32,320]{2,1,0:T(8,128)S(1)} %copy-done.4, f32[8,6,32,320]{3,2,1,0:T(8,128)S(1)} %copy-done.1, ...), custom_call_target="tpu_custom_call" | custom-call | tf_op jit(solution)/shard_map/edge/pallas_call | solution.py:369
Async XLA Ops:
  0.0 1.3 %copy-start.2 = (f32[4,6,32,320]{3,2,1,0:T(8,128)S(1)}, f32[4,6,32,320]{3,2,1,0:T(8,128)}, u32[]{:S(2)}) copy-start(f32[4,6,32,320]{3,2,1,0:T(8,128)} %a_0_.7) | copy-start | bytes 2949124
  1.3 5.5 %copy-start.3 = (s32[6,32,320]{2,1,0:T(8,128)S(1)}, s32[6,32,320]{2,1,0:T(8,128)}, u32[]{:S(2)}) copy-start(s32[6,32,320]{2,1,0:T(8,128)} %a_2_.5) | copy-start | bytes 737284
  1.3 5.5 %copy-start.4 = (s32[6,32,320]{2,1,0:T(8,128)S(1)}, s32[6,32,320]{2,1,0:T(8,128)}, u32[]{:S(2)}) copy-start(s32[6,32,320]{2,1,0:T(8,128)} %a_3_.5) | copy-start | bytes 737284
  1.5 10.2 %collective-permute-start = (f32[6,8,128]{2,1,0:T(8,128)S(1)}, f32[6,8,128]{2,1,0:T(8,128)S(1)}, u32[]{:S(2)}, u32[]{:S(2)}) collective-permute-start(f32[6,8,128]{2,1,0:T(8,128)S(1)} %get-tuple-element.9), channel_id=1, source_target_pairs={{0,1},{1,2},{2,3},{3,0},{4,5},{5,6},{6,7},{7,4},{8,9},{9,10},{10,1... | collective-permute-start | bytes 73736 | tf_op jit(solution)/shard_map/ppermute | solution.py:333
  4.6 7.1 %collective-permute-start.1 = (f32[6,8,128]{2,1,0:T(8,128)S(1)}, f32[6,8,128]{2,1,0:T(8,128)S(1)}, u32[]{:S(2)}, u32[]{:S(2)}) collective-permute-start(f32[6,8,128]{2,1,0:T(8,128)S(1)} %get-tuple-element.10), channel_id=1, source_target_pairs={{1,0},{2,1},{3,2},{0,3},{5,4},{6,5},{7,6},{4,7},{9,8},{10,9},{11,1... | collective-permute-start | bytes 73736 | tf_op jit(solution)/shard_map/ppermute | solution.py:334
  6.7 1.7 %copy-start = (f32[8,6,32,320]{3,2,1,0:T(8,128)S(1)}, f32[8,6,32,320]{3,2,1,0:T(8,128)}, u32[]{:S(2)}) copy-start(f32[8,6,32,320]{3,2,1,0:T(8,128)} %a_4_.1) | copy-start | bytes 5898244
  8.4 6.9 %copy-start.1 = (f32[8,6,32,320]{3,2,1,0:T(8,128)S(1)}, f32[8,6,32,320]{3,2,1,0:T(8,128)}, u32[]{:S(2)}) copy-start(f32[8,6,32,320]{3,2,1,0:T(8,128)} %a_4_.1) | copy-start | bytes 5898244
  12.3 10.4 %collective-permute-start.2 = (f32[4,6,4,384]{3,2,1,0:T(4,128)S(1)}, f32[4,6,4,384]{3,2,1,0:T(4,128)S(1)}, u32[]{:S(2)}, u32[]{:S(2)}) collective-permute-start(f32[4,6,4,384]{3,2,1,0:T(4,128)S(1)} %get-tuple-element.11), channel_id=1, source_target_pairs={{0,4},{4,8},{8,12},{12,16},{16,20},{20,24},{24,28},{28,30},{1,5},{... | collective-permute-start | bytes 442376 | tf_op jit(solution)/shard_map/ppermute | solution.py:356
  12.4 10.3 %collective-permute-start.3 = (f32[4,6,4,384]{3,2,1,0:T(4,128)S(1)}, f32[4,6,4,384]{3,2,1,0:T(4,128)S(1)}, u32[]{:S(2)}, u32[]{:S(2)}) collective-permute-start(f32[4,6,4,384]{3,2,1,0:T(4,128)S(1)} %get-tuple-element.12), channel_id=1, source_target_pairs={{4,0},{8,4},{12,8},{16,12},{20,16},{24,20},{28,24},{30,28},{5,1},{... | collective-permute-start | bytes 442376 | tf_op jit(solution)/shard_map/ppermute | solution.py:357

commit v3 on v2

--- a/solution.py
+++ b/solution.py
@@ -121,15 +121,16 @@
                 ccw_ref[f, l, :, q * LANES : (q + 1) * LANES] = jnp.where(low, v, s)[:HALO]
 
 
-def tile_loop(s_ref, base, rt, kr, kc, w, nf, emit):
+def tile_loop(s_ref, rt, kr, kc, w, nf, emit, build):
     r = expand(kr, w[:4])
     c = expand(kc, w[4:])
     for f in range(nf):
+        build(f)
         total = None
         for s in range(TAPS):
             line = None
             for t in range(TAPS):
-                term = c[t] * s_ref[base(f), t, pl.ds(rt * SUB + HALO + s, SUB), :]
+                term = c[t] * s_ref[f, t, pl.ds(rt * SUB + HALO + s, SUB), :]
                 line = term if line is None else line + term
             line = r[s] * line
             total = line if total is None else total + line
@@ -144,64 +145,90 @@
             s_ref[i, t, SUB + rows : 2 * SUB + rows, :] = zero
 
 
-def inner_kernel(x_ref, row_ref, col_ref, w_ref, o_ref, s_ref, *, rows, cols, rem, n, total_cols):
+def inner_kernel(
+    x_ref, row_ref, col_ref, w_hbm, o_ref, s0_ref, s1_ref, w_ref, sems, *, rows, cols, rem, n, total_cols
+):
     nf, nl = x_ref.shape[:2]
     tiles = rows // SUB
     row0 = lax.axis_index("lat") * rows
     col0 = lax.axis_index("lon") * cols + LANES
     mid = slice(LANES, 2 * LANES)
-    clear_margins(s_ref, rows)
-
-    def level(l, carry):
-        for f in range(nf):
-            for rt in range(tiles):
-                x = [tile(x_ref, (f, l), rt * SUB, q, n, rem) for q in range(n)]
-                for t in range(TAPS):
-                    s_ref[f, t, SUB + rt * SUB : 2 * SUB + rt * SUB, :] = shifted(x[0], x[1], x[2], t)
-
-        def step(rt, carry):
-            at = pl.ds(pl.multiple_of(rt * SUB, SUB), SUB)
-            kr = row_ref[l, at, mid] - (row0 + rt * SUB - HALO) - iota(0)
-            kc = col_first(col_ref[l, at, mid], col0, total_cols)
-            w = [w_ref[b, l, at, mid] for b in range(8)]
-
-            def emit(f, v):
-                o_ref[f, l, at, :] = v
-
-            tile_loop(s_ref, lambda f: f, rt, kr, kc, w, nf, emit)
-            return carry
-
-        return lax.fori_loop(0, tiles, step, carry)
-
-    lax.fori_loop(0, nl, level, 0)
+
+    def fetch(l):
+        return pltpu.make_async_copy(w_hbm.at[:, l, :, pl.ds(LANES, LANES)], w_ref.at[l], sems.at[l])
+
+    for l in range(nl):
+        fetch(l).start()
+    clear_margins(s0_ref, rows)
+    clear_margins(s1_ref, rows)
+
+    def build(s_ref, l, rt, f):
+        row = rt * SUB if isinstance(rt, int) else pl.multiple_of(rt * SUB, SUB)
+        x = [tile(x_ref, (f, l), row, q, n, rem) for q in range(n)]
+        for t in range(TAPS):
+            s_ref[f, t, pl.ds(row + SUB, SUB), :] = shifted(x[0], x[1], x[2], t)
+
+    for f in range(nf):
+        for rt in range(tiles):
+            build(s0_ref, 0, rt, f)
+
+    def pair(p, carry):
+        for side, (now, then) in enumerate(((s0_ref, s1_ref), (s1_ref, s0_ref))):
+            l = 2 * p + side
+            ahead = jnp.minimum(l + 1, nl - 1)
+            fetch(l).wait()
+
+            def step(rt, carry):
+                at = pl.ds(pl.multiple_of(rt * SUB, SUB), SUB)
+                kr = row_ref[l, at, mid] - (row0 + rt * SUB - HALO) - iota(0)
+                kc = col_first(col_ref[l, at, mid], col0, total_cols)
+                w = [w_ref[l, b, at, :] for b in range(8)]
+
+                def emit(f, v):
+                    o_ref[f, l, at, :] = v
+
+                tile_loop(now, rt, kr, kc, w, nf, emit, lambda f: build(then, ahead, rt, f))
+                return carry
+
+            lax.fori_loop(0, tiles, step, 0)
+        return carry
+
+    lax.fori_loop(0, nl // 2, pair, 0)
 
 
 def outer_kernel(
-    x_ref, row_ref, col_ref, w_ref, west_ref, east_ref, o_ref, s_ref, *, rows, cols, rem, n, total_cols
+    x_ref, row_ref, col_ref, w_ref, west_ref, east_ref, o_ref, s0_ref, s1_ref, *, rows, cols, rem, n, total_cols
 ):
     nf, nl = x_ref.shape[:2]
     tiles = rows // SUB
     row0 = lax.axis_index("lat") * rows
     col0 = lax.axis_index("lon") * cols
-    clear_margins(s_ref, rows)
+    clear_margins(s0_ref, rows)
+    clear_margins(s1_ref, rows)
+
+    def build(s_ref, side, l, rt, f):
+        row = rt * SUB if isinstance(rt, int) else pl.multiple_of(rt * SUB, SUB)
+        m = HALO * (f * tiles + rt)
+        if side:
+            prev = tile(x_ref, (f, l), row, n - 2, n, rem)
+            last = tile(x_ref, (f, l), row, n - 1, n, rem)
+            cur = jnp.where(iota(1) < rem, last, pltpu.roll(east_ref[l], (rem + LANES - m) % LANES, 1))
+            nxt = None
+        else:
+            prev = pltpu.roll(west_ref[l], (2 * LANES - HALO - m) % LANES, 1)
+            cur = tile(x_ref, (f, l), row, 0, n, rem)
+            nxt = tile(x_ref, (f, l), row, 1, n, rem)
+        for t in range(TAPS):
+            s_ref[f, t, pl.ds(row + SUB, SUB), :] = shifted(prev, cur, nxt, t)
+
+    for f in range(nf):
+        for rt in range(tiles):
+            build(s0_ref, 0, 0, rt, f)
 
     def level(l, carry):
-        west, east = west_ref[l], east_ref[l]
-        for side, q in enumerate((0, n - 1)):
-            for f in range(nf):
-                for rt in range(tiles):
-                    slot = f * tiles + rt
-                    prev, nxt = None, None
-                    if q:
-                        prev = tile(x_ref, (f, l), rt * SUB, n - 2, n, rem)
-                        cur = halo_tiles(west, east, slot, tile(x_ref, (f, l), rt * SUB, n - 1, n, rem), rem)[1]
-                    else:
-                        cur = tile(x_ref, (f, l), rt * SUB, 0, n, rem)
-                        nxt = tile(x_ref, (f, l), rt * SUB, 1, n, rem)
-                        prev = halo_tiles(west, east, slot, cur, rem)[0]
-                    to = slice(SUB + rt * SUB, 2 * SUB + rt * SUB)
-                    for t in range(TAPS):
-                        s_ref[f, t, to, :] = shifted(prev, cur, nxt, t)
+        for side, (now, then) in enumerate(((s0_ref, s1_ref), (s1_ref, s0_ref))):
+            q = side * (n - 1)
+            ahead = jnp.minimum(l + side, nl - 1)
 
             def step(rt, carry):
                 row = pl.multiple_of(rt * SUB, SUB)
@@ -213,7 +240,7 @@
                 def emit(f, v):
                     o_ref[f, l, at, side * LANES : (side + 1) * LANES] = v
 
-                tile_loop(s_ref, lambda f: f, rt, kr, kc, w, nf, emit)
+                tile_loop(now, rt, kr, kc, w, nf, emit, lambda f: build(then, 1 - side, ahead, rt, f))
                 return carry
 
             lax.fori_loop(0, tiles, step, 0)
@@ -313,7 +340,7 @@
     wide = n * LANES
     half = lon // 2
     total_cols = cols * lon
-    assert n == 3 and HALO <= rem <= LANES - HALO and rows % SUB == 0
+    assert n == 3 and nl % 2 == 0 and HALO <= rem <= LANES - HALO and rows % SUB == 0
     f32 = jnp.float32
     shape = jax.ShapeDtypeStruct
     params = lambda: pltpu.CompilerParams(vmem_limit_bytes=VMEM)
@@ -333,12 +360,13 @@
     west = lax.ppermute(west_out, "lon", up)
     east = lax.ppermute(east_out, "lon", [(j, i) for i, j in up])
 
+    shifts = pltpu.VMEM((nf, TAPS, rows + 2 * SUB, LANES), f32)
     mid = pl.pallas_call(
         lambda *a: inner_kernel(*a, rows=rows, cols=cols, rem=rem, n=n, total_cols=total_cols),
-        in_specs=[vmem] * 4,
+        in_specs=[vmem] * 3 + [pl.BlockSpec(memory_space=pltpu.HBM)],
         out_specs=vmem,
         out_shape=shape((nf, nl, rows, LANES), f32),
-        scratch_shapes=[pltpu.VMEM((nf, TAPS, rows + 2 * SUB, LANES), f32)],
+        scratch_shapes=[shifts, shifts, pltpu.VMEM((nl, 8, rows, LANES), f32), pltpu.SemaphoreType.DMA((nl,))],
         compiler_params=params(),
         name="inner",
     )(fields, dep_row, dep_col, weights)
@@ -361,7 +389,7 @@
         in_specs=[vmem] * 6,
         out_specs=vmem,
         out_shape=shape((nf, nl, rows, 2 * LANES), f32),
-        scratch_shapes=[pltpu.VMEM((nf, TAPS, rows + 2 * SUB, LANES), f32)],
+        scratch_shapes=[shifts, shifts],
         compiler_params=params(),
         name="outer",
     )(fields, dep_row, dep_col, weights, west, east)

time: 26.2 us -> 29.5 us (1.13)
  Pallas kernels: 14.8 us -> 18.1 us
    pallas_call x1, Pallas kernels: 3.3 us -> 5.05 us  [body(): pl.pallas_call(lambda *a: inner_kernel(*a, rows=rows, cols=cols, rem=rem,...]
    pallas_call x1, Pallas kernels: 7.39 us -> 8.89 us  [body(): pl.pallas_call(lambda *a: outer_kernel(*a, rows=rows, cols=cols, rem=rem,...]
  transfers between devices with their start and end apart: 4 -> 4, of which waited for: 0 -> 0; matrix products, arithmetic and copies ran while one was open for 0% -> 0% of each run, Pallas kernels for 41% -> 48%
where the time goes in v3:
time: 29.5 us; the launch traced here: 29.3 us
  Pallas kernels  18.1 us (61%)
  starting transfers between devices  8.17 us (28%)
  local copies, waits for them, and re-layouts  2.95 us (10%)
    pallas_call x1, Pallas kernels, body(): pl.pallas_call(lambda *a: outer_kernel(*a, rows=rows, cols=cols, rem=rem,...  8.89 us
    pallas_call x1, Pallas kernels, body(): pl.pallas_call(lambda *a: inner_kernel(*a, rows=rows, cols=cols, rem=rem,...  5.05 us
    pallas_call x1, Pallas kernels, body(): pl.pallas_call(lambda *a: edge_kernel(*a, rows=rows, cols=cols, rem=rem,...  3.33 us
    ppermute x1, starting transfers between devices, body(): west = lax.ppermute(west_out, 'lon', up)  3.1 us
    unnamed x10, local copies, waits for them, and re-layouts  2.95 us
    ppermute x1, starting transfers between devices, body(): ccw = lax.ppermute(ccw, ('lat', 'lon'), [(j, i) for i, j in ring])  2.91 us
    ppermute x1, starting transfers between devices, body(): east = lax.ppermute(east_out, 'lon', [(j, i) for i, j in up])  2.09 us
  transfers between devices with their start and end apart: 4, of which 0 were waited for; matrix products, arithmetic and copies ran while one was open for 0% of the time, Pallas kernels for 48%

profile of v3, /device:TPU:0, one launch (start us, length us, event | category | flops | bytes accessed | tf_op | source)
XLA Modules:
  0.0 29.3 jit_solution(13175023458811542317)
XLA Ops:
  0.0 0.0 copy-start.2
  0.0 1.3 %copy-done.2 = f32[4,6,32,320]{3,2,1,0:T(8,128)S(1)} copy-done((f32[4,6,32,320]{3,2,1,0:T(8,128)S(1)}, f32[4,6,32,320]{3,2,1,0:T(8,128)}, u32[]{:S(2)}) %copy-start.2) | copy-done | bytes 983064
  1.3 0.0 copy-start.3
  1.3 0.0 copy-start.4
  1.3 0.3 pack.1
  1.5 3.1 %collective-permute-start = (f32[6,8,128]{2,1,0:T(8,128)S(1)}, f32[6,8,128]{2,1,0:T(8,128)S(1)}, u32[]{:S(2)}, u32[]{:S(2)}) collective-permute-start(f32[6,8,128]{2,1,0:T(8,128)S(1)} %get-tuple-element.9), channel_id=1, source_target_pairs={{0,1},{1,2},{2,3},{3,0},{4,5},{5,6},{6,7},{7,4},{8,9},{9,10},{10,1... | collective-permute-start | bytes 73736 | tf_op jit(solution)/shard_map/ppermute | solution.py:360
  4.6 2.1 %collective-permute-start.1 = (f32[6,8,128]{2,1,0:T(8,128)S(1)}, f32[6,8,128]{2,1,0:T(8,128)S(1)}, u32[]{:S(2)}, u32[]{:S(2)}) collective-permute-start(f32[6,8,128]{2,1,0:T(8,128)S(1)} %get-tuple-element.10), channel_id=1, source_target_pairs={{1,0},{2,1},{3,2},{0,3},{5,4},{6,5},{7,6},{4,7},{9,8},{10,9},{11,1... | collective-permute-start | bytes 73736 | tf_op jit(solution)/shard_map/ppermute | solution.py:361
  6.7 0.0 copy-done.3
  6.7 0.0 copy-done.4
  6.7 0.0 copy-start
  6.7 1.7 %copy-done = f32[8,6,32,320]{3,2,1,0:T(8,128)S(1)} copy-done((f32[8,6,32,320]{3,2,1,0:T(8,128)S(1)}, f32[8,6,32,320]{3,2,1,0:T(8,128)}, u32[]{:S(2)}) %copy-start) | copy-done | bytes 1966104
  8.4 0.0 copy-start.1
  8.4 5.1 %inner.1.a_3_.a_5_ = f32[4,6,32,128]{3,2,1,0:T(8,128)S(1)} custom-call(f32[4,6,32,320]{3,2,1,0:T(8,128)S(1)} %copy-done.2, s32[6,32,320]{2,1,0:T(8,128)S(1)} %copy-done.3, s32[6,32,320]{2,1,0:T(8,128)S(1)} %copy-done.4, f32[8,6,32,320]{3,2,1,0:T(8,128)S(1)} %copy-done), custom_call_target="tpu_custom_call" | custom-call | tf_op jit(solution)/shard_map/inner/pallas_call | solution.py:364
  13.5 0.0 collective-permute-done.a_1_.a_4_
  13.5 0.0 collective-permute-done.1.a_2_.a_5_
  13.5 0.6 %rowpack.1 = (f32[4,6,4,384]{3,2,1,0:T(4,128)S(1)}, f32[4,6,4,384]{3,2,1,0:T(4,128)S(1)}) custom-call(f32[4,6,32,320]{3,2,1,0:T(8,128)S(1)} %copy-done.2, f32[6,8,128]{2,1,0:T(8,128)S(1)} %collective-permute-done.a_1_.a_4_, f32[6,8,128]{2,1,0:T(8,128)S(1)} %collective-permute-done.1.a_2_.a_5_, f32[4,6,32,128]{3,2,1,0:T(8,128)S(1)} %inner.1.a_3_.a_5_), custom_call_target="tpu_custom_call" | custom-call | tf_op jit(solution)/shard_map/rowpack/pallas_call | solution.py:375
  14.1 0.1 collective-permute-start.2
  14.1 2.9 %collective-permute-start.3 = (f32[4,6,4,384]{3,2,1,0:T(4,128)S(1)}, f32[4,6,4,384]{3,2,1,0:T(4,128)S(1)}, u32[]{:S(2)}, u32[]{:S(2)}) collective-permute-start(f32[4,6,4,384]{3,2,1,0:T(4,128)S(1)} %get-tuple-element.12), channel_id=1, source_target_pairs={{4,0},{8,4},{12,8},{16,12},{20,16},{24,20},{28,24},{30,28},{5,1},{... | collective-permute-start | bytes 442376 | tf_op jit(solution)/shard_map/ppermute | solution.py:385
  17.0 0.0 copy-done.1
  17.0 8.9 %outer.1.a_6_ = f32[4,6,32,256]{3,2,1,0:T(8,128)S(1)} custom-call(f32[4,6,32,320]{3,2,1,0:T(8,128)S(1)} %copy-done.2, s32[6,32,320]{2,1,0:T(8,128)S(1)} %copy-done.3, s32[6,32,320]{2,1,0:T(8,128)S(1)} %copy-done.4, f32[8,6,32,320]{3,2,1,0:T(8,128)S(1)} %copy-done.1, f32[6,8,128]{2,1,0:T(8,128)S(1)} %collective-permute-done.a_1_.a_4_, ...), custom_call_target="tpu_custom_call" | custom-call | tf_op jit(solution)/shard_map/outer/pallas_call | solution.py:387
  25.9 0.0 collective-permute-done.2.a_0_
  25.9 0.0 collective-permute-done.3.a_1_
  26.0 3.3 %edge.1 = f32[4,6,32,320]{3,2,1,0:T(8,128)} custom-call(f32[4,6,4,384]{3,2,1,0:T(4,128)S(1)} %collective-permute-done.2.a_0_, f32[4,6,4,384]{3,2,1,0:T(4,128)S(1)} %collective-permute-done.3.a_1_, s32[6,32,320]{2,1,0:T(8,128)S(1)} %copy-done.3, s32[6,32,320]{2,1,0:T(8,128)S(1)} %copy-done.4, f32[8,6,32,320]{3,2,1,0:T(8,128)S(1)} %copy-done.1, ...), custom_call_target="tpu_custom_call" | custom-call | tf_op jit(solution)/shard_map/edge/pallas_call | solution.py:397
Async XLA Ops:
  0.0 1.3 %copy-start.2 = (f32[4,6,32,320]{3,2,1,0:T(8,128)S(1)}, f32[4,6,32,320]{3,2,1,0:T(8,128)}, u32[]{:S(2)}) copy-start(f32[4,6,32,320]{3,2,1,0:T(8,128)} %a_0_.7) | copy-start | bytes 2949124
  1.3 5.5 %copy-start.3 = (s32[6,32,320]{2,1,0:T(8,128)S(1)}, s32[6,32,320]{2,1,0:T(8,128)}, u32[]{:S(2)}) copy-start(s32[6,32,320]{2,1,0:T(8,128)} %a_2_.5) | copy-start | bytes 737284
  1.3 5.5 %copy-start.4 = (s32[6,32,320]{2,1,0:T(8,128)S(1)}, s32[6,32,320]{2,1,0:T(8,128)}, u32[]{:S(2)}) copy-start(s32[6,32,320]{2,1,0:T(8,128)} %a_3_.5) | copy-start | bytes 737284
  1.5 11.9 %collective-permute-start = (f32[6,8,128]{2,1,0:T(8,128)S(1)}, f32[6,8,128]{2,1,0:T(8,128)S(1)}, u32[]{:S(2)}, u32[]{:S(2)}) collective-permute-start(f32[6,8,128]{2,1,0:T(8,128)S(1)} %get-tuple-element.9), channel_id=1, source_target_pairs={{0,1},{1,2},{2,3},{3,0},{4,5},{5,6},{6,7},{7,4},{8,9},{9,10},{10,1... | collective-permute-start | bytes 73736 | tf_op jit(solution)/shard_map/ppermute | solution.py:360
  4.6 8.8 %collective-permute-start.1 = (f32[6,8,128]{2,1,0:T(8,128)S(1)}, f32[6,8,128]{2,1,0:T(8,128)S(1)}, u32[]{:S(2)}, u32[]{:S(2)}) collective-permute-start(f32[6,8,128]{2,1,0:T(8,128)S(1)} %get-tuple-element.10), channel_id=1, source_target_pairs={{1,0},{2,1},{3,2},{0,3},{5,4},{6,5},{7,6},{4,7},{9,8},{10,9},{11,1... | collective-permute-start | bytes 73736 | tf_op jit(solution)/shard_map/ppermute | solution.py:361
  6.7 1.7 %copy-start = (f32[8,6,32,320]{3,2,1,0:T(8,128)S(1)}, f32[8,6,32,320]{3,2,1,0:T(8,128)}, u32[]{:S(2)}) copy-start(f32[8,6,32,320]{3,2,1,0:T(8,128)} %a_4_.1) | copy-start | bytes 5898244
  8.4 8.6 %copy-start.1 = (f32[8,6,32,320]{3,2,1,0:T(8,128)S(1)}, f32[8,6,32,320]{3,2,1,0:T(8,128)}, u32[]{:S(2)}) copy-start(f32[8,6,32,320]{3,2,1,0:T(8,128)} %a_4_.1) | copy-start | bytes 5898244
  14.1 11.9 %collective-permute-start.2 = (f32[4,6,4,384]{3,2,1,0:T(4,128)S(1)}, f32[4,6,4,384]{3,2,1,0:T(4,128)S(1)}, u32[]{:S(2)}, u32[]{:S(2)}) collective-permute-start(f32[4,6,4,384]{3,2,1,0:T(4,128)S(1)} %get-tuple-element.11), channel_id=1, source_target_pairs={{0,4},{4,8},{8,12},{12,16},{16,20},{20,24},{24,28},{28,30},{1,5},{... | collective-permute-start | bytes 442376 | tf_op jit(solution)/shard_map/ppermute | solution.py:384
  14.1 11.8 %collective-permute-start.3 = (f32[4,6,4,384]{3,2,1,0:T(4,128)S(1)}, f32[4,6,4,384]{3,2,1,0:T(4,128)S(1)}, u32[]{:S(2)}, u32[]{:S(2)}) collective-permute-start(f32[4,6,4,384]{3,2,1,0:T(4,128)S(1)} %get-tuple-element.12), channel_id=1, source_target_pairs={{4,0},{8,4},{12,8},{16,12},{20,16},{24,20},{28,24},{30,28},{5,1},{... | collective-permute-start | bytes 442376 | tf_op jit(solution)/shard_map/ppermute | solution.py:385

commit v4 on v2

--- a/solution.py
+++ b/solution.py
@@ -338,7 +338,7 @@
         in_specs=[vmem] * 4,
         out_specs=vmem,
         out_shape=shape((nf, nl, rows, LANES), f32),
-        scratch_shapes=[pltpu.VMEM((nf, TAPS, rows + 2 * SUB, LANES), f32)],
+        scratch_shapes=[pltpu.VMEM((nf, TAPS, rows + 3 * SUB, LANES), f32)],
         compiler_params=params(),
         name="inner",
     )(fields, dep_row, dep_col, weights)
@@ -361,7 +361,7 @@
         in_specs=[vmem] * 6,
         out_specs=vmem,
         out_shape=shape((nf, nl, rows, 2 * LANES), f32),
-        scratch_shapes=[pltpu.VMEM((nf, TAPS, rows + 2 * SUB, LANES), f32)],
+        scratch_shapes=[pltpu.VMEM((nf, TAPS, rows + 3 * SUB, LANES), f32)],
         compiler_params=params(),
         name="outer",
     )(fields, dep_row, dep_col, weights, west, east)

time: 26.2 us -> 26.2 us (level)
  no operation moved by 1% of the time
where the time goes in v4:
time: 26.2 us; the launch traced here: 26 us
  Pallas kernels  14.8 us (56%)
  starting transfers between devices  8.17 us (31%)
  local copies, waits for them, and re-layouts  2.95 us (11%)
    pallas_call x1, Pallas kernels, body(): pl.pallas_call(lambda *a: outer_kernel(*a, rows=rows, cols=cols, rem=rem,...  7.37 us
    pallas_call x1, Pallas kernels, body(): pl.pallas_call(lambda *a: edge_kernel(*a, rows=rows, cols=cols, rem=rem,...  3.33 us
    pallas_call x1, Pallas kernels, body(): pl.pallas_call(lambda *a: inner_kernel(*a, rows=rows, cols=cols, rem=rem,...  3.29 us
    ppermute x1, starting transfers between devices, body(): west = lax.ppermute(west_out, 'lon', up)  3.1 us
    unnamed x10, local copies, waits for them, and re-layouts  2.95 us
    ppermute x1, starting transfers between devices, body(): ccw = lax.ppermute(ccw, ('lat', 'lon'), [(j, i) for i, j in ring])  2.91 us
    ppermute x1, starting transfers between devices, body(): east = lax.ppermute(east_out, 'lon', [(j, i) for i, j in up])  2.09 us
    pallas_call x1, Pallas kernels, body(): pl.pallas_call(lambda *a: rowpack_kernel(*a, rem=rem, tiles=tiles, n=n, h...  0.56 us
  transfers between devices with their start and end apart: 4, of which 0 were waited for; matrix products, arithmetic and copies ran while one was open for 0% of the time, Pallas kernels for 41%

profile of v4, /device:TPU:0, one launch (start us, length us, event | category | flops | bytes accessed | tf_op | source)
XLA Modules:
  0.0 26.0 jit_solution(3712318730720030004)
XLA Ops:
  0.0 0.0 copy-start.2
  0.0 1.3 %copy-done.2 = f32[4,6,32,320]{3,2,1,0:T(8,128)S(1)} copy-done((f32[4,6,32,320]{3,2,1,0:T(8,128)S(1)}, f32[4,6,32,320]{3,2,1,0:T(8,128)}, u32[]{:S(2)}) %copy-start.2) | copy-done | bytes 983064
  1.3 0.0 copy-start.3
  1.3 0.0 copy-start.4
  1.3 0.3 pack.1
  1.5 3.1 %collective-permute-start = (f32[6,8,128]{2,1,0:T(8,128)S(1)}, f32[6,8,128]{2,1,0:T(8,128)S(1)}, u32[]{:S(2)}, u32[]{:S(2)}) collective-permute-start(f32[6,8,128]{2,1,0:T(8,128)S(1)} %get-tuple-element.9), channel_id=1, source_target_pairs={{0,1},{1,2},{2,3},{3,0},{4,5},{5,6},{6,7},{7,4},{8,9},{9,10},{10,1... | collective-permute-start | bytes 73736 | tf_op jit(solution)/shard_map/ppermute | solution.py:333
  4.6 2.1 %collective-permute-start.1 = (f32[6,8,128]{2,1,0:T(8,128)S(1)}, f32[6,8,128]{2,1,0:T(8,128)S(1)}, u32[]{:S(2)}, u32[]{:S(2)}) collective-permute-start(f32[6,8,128]{2,1,0:T(8,128)S(1)} %get-tuple-element.10), channel_id=1, source_target_pairs={{1,0},{2,1},{3,2},{0,3},{5,4},{6,5},{7,6},{4,7},{9,8},{10,9},{11,1... | collective-permute-start | bytes 73736 | tf_op jit(solution)/shard_map/ppermute | solution.py:334
  6.7 0.0 copy-done.3
  6.7 0.0 copy-done.4
  6.7 0.0 copy-start
  6.7 1.7 %copy-done = f32[8,6,32,320]{3,2,1,0:T(8,128)S(1)} copy-done((f32[8,6,32,320]{3,2,1,0:T(8,128)S(1)}, f32[8,6,32,320]{3,2,1,0:T(8,128)}, u32[]{:S(2)}) %copy-start) | copy-done | bytes 1966104
  8.4 0.0 copy-start.1
  8.4 3.3 %inner.1.a_3_.a_5_ = f32[4,6,32,128]{3,2,1,0:T(8,128)S(1)} custom-call(f32[4,6,32,320]{3,2,1,0:T(8,128)S(1)} %copy-done.2, s32[6,32,320]{2,1,0:T(8,128)S(1)} %copy-done.3, s32[6,32,320]{2,1,0:T(8,128)S(1)} %copy-done.4, f32[8,6,32,320]{3,2,1,0:T(8,128)S(1)} %copy-done), custom_call_target="tpu_custom_call" | custom-call | tf_op jit(solution)/shard_map/inner/pallas_call | solution.py:336
  11.7 0.0 collective-permute-done.a_1_.a_4_
  11.7 0.0 collective-permute-done.1.a_2_.a_5_
  11.7 0.6 %rowpack.1 = (f32[4,6,4,384]{3,2,1,0:T(4,128)S(1)}, f32[4,6,4,384]{3,2,1,0:T(4,128)S(1)}) custom-call(f32[4,6,32,320]{3,2,1,0:T(8,128)S(1)} %copy-done.2, f32[6,8,128]{2,1,0:T(8,128)S(1)} %collective-permute-done.a_1_.a_4_, f32[6,8,128]{2,1,0:T(8,128)S(1)} %collective-permute-done.1.a_2_.a_5_, f32[4,6,32,128]{3,2,1,0:T(8,128)S(1)} %inner.1.a_3_.a_5_), custom_call_target="tpu_custom_call" | custom-call | tf_op jit(solution)/shard_map/rowpack/pallas_call | solution.py:347
  12.3 0.1 collective-permute-start.2
  12.4 2.9 %collective-permute-start.3 = (f32[4,6,4,384]{3,2,1,0:T(4,128)S(1)}, f32[4,6,4,384]{3,2,1,0:T(4,128)S(1)}, u32[]{:S(2)}, u32[]{:S(2)}) collective-permute-start(f32[4,6,4,384]{3,2,1,0:T(4,128)S(1)} %get-tuple-element.12), channel_id=1, source_target_pairs={{4,0},{8,4},{12,8},{16,12},{20,16},{24,20},{28,24},{30,28},{5,1},{... | collective-permute-start | bytes 442376 | tf_op jit(solution)/shard_map/ppermute | solution.py:357
  15.3 0.0 copy-done.1
  15.3 7.4 %outer.1.a_6_ = f32[4,6,32,256]{3,2,1,0:T(8,128)S(1)} custom-call(f32[4,6,32,320]{3,2,1,0:T(8,128)S(1)} %copy-done.2, s32[6,32,320]{2,1,0:T(8,128)S(1)} %copy-done.3, s32[6,32,320]{2,1,0:T(8,128)S(1)} %copy-done.4, f32[8,6,32,320]{3,2,1,0:T(8,128)S(1)} %copy-done.1, f32[6,8,128]{2,1,0:T(8,128)S(1)} %collective-permute-done.a_1_.a_4_, ...), custom_call_target="tpu_custom_call" | custom-call | tf_op jit(solution)/shard_map/outer/pallas_call | solution.py:359
  22.7 0.0 collective-permute-done.2.a_0_
  22.7 0.0 collective-permute-done.3.a_1_
  22.7 3.3 %edge.1 = f32[4,6,32,320]{3,2,1,0:T(8,128)} custom-call(f32[4,6,4,384]{3,2,1,0:T(4,128)S(1)} %collective-permute-done.2.a_0_, f32[4,6,4,384]{3,2,1,0:T(4,128)S(1)} %collective-permute-done.3.a_1_, s32[6,32,320]{2,1,0:T(8,128)S(1)} %copy-done.3, s32[6,32,320]{2,1,0:T(8,128)S(1)} %copy-done.4, f32[8,6,32,320]{3,2,1,0:T(8,128)S(1)} %copy-done.1, ...), custom_call_target="tpu_custom_call" | custom-call | tf_op jit(solution)/shard_map/edge/pallas_call | solution.py:369
Async XLA Ops:
  0.0 1.3 %copy-start.2 = (f32[4,6,32,320]{3,2,1,0:T(8,128)S(1)}, f32[4,6,32,320]{3,2,1,0:T(8,128)}, u32[]{:S(2)}) copy-start(f32[4,6,32,320]{3,2,1,0:T(8,128)} %a_0_.7) | copy-start | bytes 2949124
  1.3 5.5 %copy-start.3 = (s32[6,32,320]{2,1,0:T(8,128)S(1)}, s32[6,32,320]{2,1,0:T(8,128)}, u32[]{:S(2)}) copy-start(s32[6,32,320]{2,1,0:T(8,128)} %a_2_.5) | copy-start | bytes 737284
  1.3 5.5 %copy-start.4 = (s32[6,32,320]{2,1,0:T(8,128)S(1)}, s32[6,32,320]{2,1,0:T(8,128)}, u32[]{:S(2)}) copy-start(s32[6,32,320]{2,1,0:T(8,128)} %a_3_.5) | copy-start | bytes 737284
  1.5 10.2 %collective-permute-start = (f32[6,8,128]{2,1,0:T(8,128)S(1)}, f32[6,8,128]{2,1,0:T(8,128)S(1)}, u32[]{:S(2)}, u32[]{:S(2)}) collective-permute-start(f32[6,8,128]{2,1,0:T(8,128)S(1)} %get-tuple-element.9), channel_id=1, source_target_pairs={{0,1},{1,2},{2,3},{3,0},{4,5},{5,6},{6,7},{7,4},{8,9},{9,10},{10,1... | collective-permute-start | bytes 73736 | tf_op jit(solution)/shard_map/ppermute | solution.py:333
  4.6 7.1 %collective-permute-start.1 = (f32[6,8,128]{2,1,0:T(8,128)S(1)}, f32[6,8,128]{2,1,0:T(8,128)S(1)}, u32[]{:S(2)}, u32[]{:S(2)}) collective-permute-start(f32[6,8,128]{2,1,0:T(8,128)S(1)} %get-tuple-element.10), channel_id=1, source_target_pairs={{1,0},{2,1},{3,2},{0,3},{5,4},{6,5},{7,6},{4,7},{9,8},{10,9},{11,1... | collective-permute-start | bytes 73736 | tf_op jit(solution)/shard_map/ppermute | solution.py:334
  6.7 1.7 %copy-start = (f32[8,6,32,320]{3,2,1,0:T(8,128)S(1)}, f32[8,6,32,320]{3,2,1,0:T(8,128)}, u32[]{:S(2)}) copy-start(f32[8,6,32,320]{3,2,1,0:T(8,128)} %a_4_.1) | copy-start | bytes 5898244
  8.4 6.9 %copy-start.1 = (f32[8,6,32,320]{3,2,1,0:T(8,128)S(1)}, f32[8,6,32,320]{3,2,1,0:T(8,128)}, u32[]{:S(2)}) copy-start(f32[8,6,32,320]{3,2,1,0:T(8,128)} %a_4_.1) | copy-start | bytes 5898244
  12.3 10.4 %collective-permute-start.2 = (f32[4,6,4,384]{3,2,1,0:T(4,128)S(1)}, f32[4,6,4,384]{3,2,1,0:T(4,128)S(1)}, u32[]{:S(2)}, u32[]{:S(2)}) collective-permute-start(f32[4,6,4,384]{3,2,1,0:T(4,128)S(1)} %get-tuple-element.11), channel_id=1, source_target_pairs={{0,4},{4,8},{8,12},{12,16},{16,20},{20,24},{24,28},{28,30},{1,5},{... | collective-permute-start | bytes 442376 | tf_op jit(solution)/shard_map/ppermute | solution.py:356
  12.4 10.3 %collective-permute-start.3 = (f32[4,6,4,384]{3,2,1,0:T(4,128)S(1)}, f32[4,6,4,384]{3,2,1,0:T(4,128)S(1)}, u32[]{:S(2)}, u32[]{:S(2)}) collective-permute-start(f32[4,6,4,384]{3,2,1,0:T(4,128)S(1)} %get-tuple-element.12), channel_id=1, source_target_pairs={{4,0},{8,4},{12,8},{16,12},{20,16},{24,20},{28,24},{30,28},{5,1},{... | collective-permute-start | bytes 442376 | tf_op jit(solution)/shard_map/ppermute | solution.py:357

commit v5 on v4

--- a/solution.py
+++ b/solution.py
@@ -171,7 +171,7 @@
             tile_loop(s_ref, lambda f: f, rt, kr, kc, w, nf, emit)
             return carry
 
-        return lax.fori_loop(0, tiles, step, carry)
+        return lax.fori_loop(0, tiles, step, carry, unroll=2)
 
     lax.fori_loop(0, nl, level, 0)
 
@@ -216,7 +216,7 @@
                 tile_loop(s_ref, lambda f: f, rt, kr, kc, w, nf, emit)
                 return carry
 
-            lax.fori_loop(0, tiles, step, 0)
+            lax.fori_loop(0, tiles, step, 0, unroll=2)
         return carry
 
     lax.fori_loop(0, nl, level, 0)

time: 26.2 us -> 26 us (level)
  transfers between devices with their start and end apart: 4 -> 4, of which waited for: 0 -> 0; matrix products, arithmetic and copies ran while one was open for 0% -> 0% of each run, Pallas kernels for 41% -> 40%
where the time goes in v5:
time: 26 us; the launch traced here: 25.8 us
  Pallas kernels  14.6 us (56%)
  starting transfers between devices  8.17 us (31%)
  local copies, waits for them, and re-layouts  2.95 us (11%)
    pallas_call x1, Pallas kernels, body(): pl.pallas_call(lambda *a: outer_kernel(*a, rows=rows, cols=cols, rem=rem,...  7.28 us
    pallas_call x1, Pallas kernels, body(): pl.pallas_call(lambda *a: edge_kernel(*a, rows=rows, cols=cols, rem=rem,...  3.33 us
    pallas_call x1, Pallas kernels, body(): pl.pallas_call(lambda *a: inner_kernel(*a, rows=rows, cols=cols, rem=rem,...  3.16 us
    ppermute x1, starting transfers between devices, body(): west = lax.ppermute(west_out, 'lon', up)  3.1 us
    unnamed x10, local copies, waits for them, and re-layouts  2.95 us
    ppermute x1, starting transfers between devices, body(): ccw = lax.ppermute(ccw, ('lat', 'lon'), [(j, i) for i, j in ring])  2.91 us
    ppermute x1, starting transfers between devices, body(): east = lax.ppermute(east_out, 'lon', [(j, i) for i, j in up])  2.09 us
    pallas_call x1, Pallas kernels, body(): pl.pallas_call(lambda *a: rowpack_kernel(*a, rem=rem, tiles=tiles, n=n, h...  0.56 us
  transfers between devices with their start and end apart: 4, of which 0 were waited for; matrix products, arithmetic and copies ran while one was open for 0% of the time, Pallas kernels for 40%

profile of v5, /device:TPU:0, one launch (start us, length us, event | category | flops | bytes accessed | tf_op | source)
XLA Modules:
  0.0 25.8 jit_solution(6605587539842950495)
XLA Ops:
  0.0 0.0 copy-start.2
  0.0 1.3 %copy-done.2 = f32[4,6,32,320]{3,2,1,0:T(8,128)S(1)} copy-done((f32[4,6,32,320]{3,2,1,0:T(8,128)S(1)}, f32[4,6,32,320]{3,2,1,0:T(8,128)}, u32[]{:S(2)}) %copy-start.2) | copy-done | bytes 983064
  1.3 0.0 copy-start.3
  1.3 0.0 copy-start.4
  1.3 0.3 pack.1
  1.5 3.1 %collective-permute-start = (f32[6,8,128]{2,1,0:T(8,128)S(1)}, f32[6,8,128]{2,1,0:T(8,128)S(1)}, u32[]{:S(2)}, u32[]{:S(2)}) collective-permute-start(f32[6,8,128]{2,1,0:T(8,128)S(1)} %get-tuple-element.9), channel_id=1, source_target_pairs={{0,1},{1,2},{2,3},{3,0},{4,5},{5,6},{6,7},{7,4},{8,9},{9,10},{10,1... | collective-permute-start | bytes 73736 | tf_op jit(solution)/shard_map/ppermute | solution.py:333
  4.6 2.1 %collective-permute-start.1 = (f32[6,8,128]{2,1,0:T(8,128)S(1)}, f32[6,8,128]{2,1,0:T(8,128)S(1)}, u32[]{:S(2)}, u32[]{:S(2)}) collective-permute-start(f32[6,8,128]{2,1,0:T(8,128)S(1)} %get-tuple-element.10), channel_id=1, source_target_pairs={{1,0},{2,1},{3,2},{0,3},{5,4},{6,5},{7,6},{4,7},{9,8},{10,9},{11,1... | collective-permute-start | bytes 73736 | tf_op jit(solution)/shard_map/ppermute | solution.py:334
  6.7 0.0 copy-done.3
  6.7 0.0 copy-done.4
  6.7 0.0 copy-start
  6.7 1.7 %copy-done = f32[8,6,32,320]{3,2,1,0:T(8,128)S(1)} copy-done((f32[8,6,32,320]{3,2,1,0:T(8,128)S(1)}, f32[8,6,32,320]{3,2,1,0:T(8,128)}, u32[]{:S(2)}) %copy-start) | copy-done | bytes 1966104
  8.4 0.0 copy-start.1
  8.4 3.2 %inner.1.a_3_.a_5_ = f32[4,6,32,128]{3,2,1,0:T(8,128)S(1)} custom-call(f32[4,6,32,320]{3,2,1,0:T(8,128)S(1)} %copy-done.2, s32[6,32,320]{2,1,0:T(8,128)S(1)} %copy-done.3, s32[6,32,320]{2,1,0:T(8,128)S(1)} %copy-done.4, f32[8,6,32,320]{3,2,1,0:T(8,128)S(1)} %copy-done), custom_call_target="tpu_custom_call" | custom-call | tf_op jit(solution)/shard_map/inner/pallas_call | solution.py:336
  11.6 0.0 collective-permute-done.a_1_.a_4_
  11.6 0.0 collective-permute-done.1.a_2_.a_5_
  11.6 0.6 %rowpack.1 = (f32[4,6,4,384]{3,2,1,0:T(4,128)S(1)}, f32[4,6,4,384]{3,2,1,0:T(4,128)S(1)}) custom-call(f32[4,6,32,320]{3,2,1,0:T(8,128)S(1)} %copy-done.2, f32[6,8,128]{2,1,0:T(8,128)S(1)} %collective-permute-done.a_1_.a_4_, f32[6,8,128]{2,1,0:T(8,128)S(1)} %collective-permute-done.1.a_2_.a_5_, f32[4,6,32,128]{3,2,1,0:T(8,128)S(1)} %inner.1.a_3_.a_5_), custom_call_target="tpu_custom_call" | custom-call | tf_op jit(solution)/shard_map/rowpack/pallas_call | solution.py:347
  12.2 0.1 collective-permute-start.2
  12.2 2.9 %collective-permute-start.3 = (f32[4,6,4,384]{3,2,1,0:T(4,128)S(1)}, f32[4,6,4,384]{3,2,1,0:T(4,128)S(1)}, u32[]{:S(2)}, u32[]{:S(2)}) collective-permute-start(f32[4,6,4,384]{3,2,1,0:T(4,128)S(1)} %get-tuple-element.12), channel_id=1, source_target_pairs={{4,0},{8,4},{12,8},{16,12},{20,16},{24,20},{28,24},{30,28},{5,1},{... | collective-permute-start | bytes 442376 | tf_op jit(solution)/shard_map/ppermute | solution.py:357
  15.2 0.0 copy-done.1
  15.2 7.3 %outer.1.a_6_ = f32[4,6,32,256]{3,2,1,0:T(8,128)S(1)} custom-call(f32[4,6,32,320]{3,2,1,0:T(8,128)S(1)} %copy-done.2, s32[6,32,320]{2,1,0:T(8,128)S(1)} %copy-done.3, s32[6,32,320]{2,1,0:T(8,128)S(1)} %copy-done.4, f32[8,6,32,320]{3,2,1,0:T(8,128)S(1)} %copy-done.1, f32[6,8,128]{2,1,0:T(8,128)S(1)} %collective-permute-done.a_1_.a_4_, ...), custom_call_target="tpu_custom_call" | custom-call | tf_op jit(solution)/shard_map/outer/pallas_call | solution.py:359
  22.4 0.0 collective-permute-done.2.a_0_
  22.5 0.0 collective-permute-done.3.a_1_
  22.5 3.3 %edge.1 = f32[4,6,32,320]{3,2,1,0:T(8,128)} custom-call(f32[4,6,4,384]{3,2,1,0:T(4,128)S(1)} %collective-permute-done.2.a_0_, f32[4,6,4,384]{3,2,1,0:T(4,128)S(1)} %collective-permute-done.3.a_1_, s32[6,32,320]{2,1,0:T(8,128)S(1)} %copy-done.3, s32[6,32,320]{2,1,0:T(8,128)S(1)} %copy-done.4, f32[8,6,32,320]{3,2,1,0:T(8,128)S(1)} %copy-done.1, ...), custom_call_target="tpu_custom_call" | custom-call | tf_op jit(solution)/shard_map/edge/pallas_call | solution.py:369
Async XLA Ops:
  0.0 1.3 %copy-start.2 = (f32[4,6,32,320]{3,2,1,0:T(8,128)S(1)}, f32[4,6,32,320]{3,2,1,0:T(8,128)}, u32[]{:S(2)}) copy-start(f32[4,6,32,320]{3,2,1,0:T(8,128)} %a_0_.7) | copy-start | bytes 2949124
  1.3 5.5 %copy-start.3 = (s32[6,32,320]{2,1,0:T(8,128)S(1)}, s32[6,32,320]{2,1,0:T(8,128)}, u32[]{:S(2)}) copy-start(s32[6,32,320]{2,1,0:T(8,128)} %a_2_.5) | copy-start | bytes 737284
  1.3 5.5 %copy-start.4 = (s32[6,32,320]{2,1,0:T(8,128)S(1)}, s32[6,32,320]{2,1,0:T(8,128)}, u32[]{:S(2)}) copy-start(s32[6,32,320]{2,1,0:T(8,128)} %a_3_.5) | copy-start | bytes 737284
  1.5 10.0 %collective-permute-start = (f32[6,8,128]{2,1,0:T(8,128)S(1)}, f32[6,8,128]{2,1,0:T(8,128)S(1)}, u32[]{:S(2)}, u32[]{:S(2)}) collective-permute-start(f32[6,8,128]{2,1,0:T(8,128)S(1)} %get-tuple-element.9), channel_id=1, source_target_pairs={{0,1},{1,2},{2,3},{3,0},{4,5},{5,6},{6,7},{7,4},{8,9},{9,10},{10,1... | collective-permute-start | bytes 73736 | tf_op jit(solution)/shard_map/ppermute | solution.py:333
  4.6 7.0 %collective-permute-start.1 = (f32[6,8,128]{2,1,0:T(8,128)S(1)}, f32[6,8,128]{2,1,0:T(8,128)S(1)}, u32[]{:S(2)}, u32[]{:S(2)}) collective-permute-start(f32[6,8,128]{2,1,0:T(8,128)S(1)} %get-tuple-element.10), channel_id=1, source_target_pairs={{1,0},{2,1},{3,2},{0,3},{5,4},{6,5},{7,6},{4,7},{9,8},{10,9},{11,1... | collective-permute-start | bytes 73736 | tf_op jit(solution)/shard_map/ppermute | solution.py:334
  6.7 1.7 %copy-start = (f32[8,6,32,320]{3,2,1,0:T(8,128)S(1)}, f32[8,6,32,320]{3,2,1,0:T(8,128)}, u32[]{:S(2)}) copy-start(f32[8,6,32,320]{3,2,1,0:T(8,128)} %a_4_.1) | copy-start | bytes 5898244
  8.4 6.8 %copy-start.1 = (f32[8,6,32,320]{3,2,1,0:T(8,128)S(1)}, f32[8,6,32,320]{3,2,1,0:T(8,128)}, u32[]{:S(2)}) copy-start(f32[8,6,32,320]{3,2,1,0:T(8,128)} %a_4_.1) | copy-start | bytes 5898244
  12.2 10.3 %collective-permute-start.2 = (f32[4,6,4,384]{3,2,1,0:T(4,128)S(1)}, f32[4,6,4,384]{3,2,1,0:T(4,128)S(1)}, u32[]{:S(2)}, u32[]{:S(2)}) collective-permute-start(f32[4,6,4,384]{3,2,1,0:T(4,128)S(1)} %get-tuple-element.11), channel_id=1, source_target_pairs={{0,4},{4,8},{8,12},{12,16},{16,20},{20,24},{24,28},{28,30},{1,5},{... | collective-permute-start | bytes 442376 | tf_op jit(solution)/shard_map/ppermute | solution.py:356
  12.2 10.2 %collective-permute-start.3 = (f32[4,6,4,384]{3,2,1,0:T(4,128)S(1)}, f32[4,6,4,384]{3,2,1,0:T(4,128)S(1)}, u32[]{:S(2)}, u32[]{:S(2)}) collective-permute-start(f32[4,6,4,384]{3,2,1,0:T(4,128)S(1)} %get-tuple-element.12), channel_id=1, source_target_pairs={{4,0},{8,4},{12,8},{16,12},{20,16},{24,20},{28,24},{30,28},{5,1},{... | collective-permute-start | bytes 442376 | tf_op jit(solution)/shard_map/ppermute | solution.py:357
